TPU v7x, 128 devices: a whole 4x4x4 slice. The times are simulated.
128 devices in a mesh: cls: 128 (over y, x, z, core).
Axes of the slice: x: 4, y: 4, z: 4, core: 2. Of those that a mesh axis runs over, the one named last changes fastest.
Arguments:
- features: bfloat16 [2048, 12544], P('cls'), may hold values from -6 to 6
- fc_weight: bfloat16 [12544, 512], replicated, may hold values from -0.0546875 to 0.0546875
- centers: bfloat16 [524288, 512], P('cls'), may hold values from -6 to 6
- labels: int32 [2048], replicated, may hold values from 0 to 524287
Outputs:
- loss: float32 [2048], P('cls')
- grad_centers: bfloat16 [524288, 512], P('cls')
- grad_fc: float32 [12544, 512], P('cls')
All inputs are finite; a program needn't handle non-finite values.
Results may differ from a plain program's by a relative error of at most 0.0078.
Values may be sent and summed in bfloat16 or wider, within the bound.
A program may use at most 128 MiB of HBM per device.

v0:
```python
import math

import jax
import jax.numpy as jnp
from jax import lax
from jax.sharding import Mesh
from jax.sharding import PartitionSpec as P

CLS = ("cls_0", "cls_1", "cls_2", "cls_3")


logit_scale = 64.0
cos_margin = math.cos(0.5)
sin_margin = math.sin(0.5)
epsilon = 1e-06


def from_everyone(x, axis):
    copies = jnp.broadcast_to(x, (lax.axis_size(axis), *x.shape))
    return lax.all_to_all(copies, axis, split_axis=0, concat_axis=0, tiled=True)


def joined_along(tiles, dim):
    shape = list(tiles.shape[1:])
    shape[dim] *= tiles.shape[0]
    return jnp.moveaxis(tiles, 0, dim).reshape(shape)


def gathered_by_axis(x, axes, dim):
    far, near = axes
    tiles = from_everyone(from_everyone(x, far), near)
    return joined_along(tiles.swapaxes(0, 1).reshape(-1, *x.shape), dim)


def of_everyone(x, axis):
    return from_everyone(x, axis).sum(axis=0)


def by_axis(x, axes):
    far, near = axes
    return of_everyone(of_everyone(x, near), far)


def in_one(arrays, axis):
    ends = [0]
    for a in arrays:
        ends.append(ends[-1] + a.size)
    subtotal = by_axis(jnp.concatenate([a.ravel() for a in arrays]), axis)
    return tuple((subtotal[b:e].reshape(a.shape) for a, b, e in zip(arrays, ends, ends[1:])))


def cut_along(x, dim, peers):
    shape = x.shape
    tiles = x.reshape(*shape[:dim], peers, shape[dim] // peers, *shape[dim + 1 :])
    return jnp.moveaxis(tiles, dim, 0)


def summed_on_arrival(x, axis, dim):
    peers = lax.axis_size(axis)
    tiles = lax.all_to_all(cut_along(x, dim, peers), axis, 0, 0, tiled=True)
    return jnp.sum(tiles.astype(jnp.float32), axis=0)


def sum_by_axis(x, axes, dim):
    far, near = axes
    own = summed_on_arrival(cut_along(x, dim, lax.axis_size(far)), near, dim + 1)
    return jnp.sum(
        lax.all_to_all(own.astype(jnp.bfloat16), far, 0, 0, tiled=True).astype(jnp.float32), axis=0
    )


def inverse_norm(values):
    return lax.rsqrt(jnp.sum(values * values, axis=1, keepdims=True) + epsilon)


def margin_logits(emb_low, center_low, labels, offset):
    cosines = lax.dot_general(
        emb_low, center_low, (((1,), (1,)), ((), ())), preferred_element_type=jnp.float32
    )
    local_ids = labels - offset
    is_target = local_ids[:, None] == lax.broadcasted_iota(jnp.int32, (1, center_low.shape[0]), 1)
    target_cos = jnp.sum(jnp.where(is_target, cosines, 0.0), axis=1)
    target_sine = jnp.sqrt(1.0 - target_cos * target_cos)
    margined = target_cos * cos_margin - target_sine * sin_margin
    logits = logit_scale * jnp.where(is_target, margined[:, None], cosines)
    slope = cos_margin + sin_margin * target_cos / target_sine
    return (logits, is_target, slope)


def on_device(features, fc_weight, centers, labels):
    tok_rows = features.shape[0]
    class_rows = centers.shape[0]
    my_index = lax.axis_index(CLS)
    columns = lax.all_to_all(features, CLS, split_axis=1, concat_axis=0, tiled=True)
    embedded = jnp.dot(features, fc_weight, preferred_element_type=jnp.float32).astype(jnp.bfloat16)
    gathered = gathered_by_axis(embedded, (("cls_0", "cls_1", "cls_2"), "cls_3"), 0)
    all_float = gathered.astype(jnp.float32)
    emb_low = (all_float * inverse_norm(all_float)).astype(jnp.bfloat16)
    own_float = embedded.astype(jnp.float32)
    inv_emb = inverse_norm(own_float)
    emb_dir = own_float * inv_emb
    center_float = centers.astype(jnp.float32)
    inv_center = inverse_norm(center_float)
    center_dir = center_float * inv_center
    center_low = center_dir.astype(jnp.bfloat16)
    logits, is_target, slope = margin_logits(emb_low, center_low, labels, my_index * class_rows)
    target_logit = jnp.sum(jnp.where(is_target, logits, 0.0), axis=1)
    row_total, target_all = in_one(
        (jnp.sum(jnp.exp(logits - logit_scale), axis=1), target_logit),
        (("cls_0", "cls_1"), ("cls_2", "cls_3")),
    )
    log_total = logit_scale + jnp.log(row_total)
    loss = lax.dynamic_slice_in_dim(log_total - target_all, my_index * tok_rows, tok_rows)
    probs = jnp.exp(logits - log_total[:, None])
    grad_cos = (
        logit_scale
        * (probs - is_target.astype(jnp.float32))
        * jnp.where(is_target, slope[:, None], 1.0)
    ).astype(jnp.bfloat16)
    grad_unit = lax.dot_general(
        grad_cos, emb_low, (((0,), (0,)), ((), ())), preferred_element_type=jnp.float32
    )
    grad_centers = (
        (grad_unit - center_dir * jnp.sum(grad_unit * center_dir, axis=1, keepdims=True))
        * inv_center
    ).astype(jnp.bfloat16)
    grad_dir = sum_by_axis(
        jnp.dot(grad_cos, center_low, preferred_element_type=jnp.float32).astype(jnp.bfloat16),
        (("cls_0", "cls_1", "cls_2"), "cls_3"),
        0,
    )
    grad_emb = (
        (grad_dir - emb_dir * jnp.sum(grad_dir * emb_dir, axis=1, keepdims=True)) * inv_emb
    ).astype(jnp.bfloat16)
    all_grads = gathered_by_axis(grad_emb, (("cls_0", "cls_1", "cls_2"), "cls_3"), 0)
    grad_fc = lax.dot_general(
        columns, all_grads, (((0,), (0,)), ((), ())), preferred_element_type=jnp.float32
    )
    return (loss, grad_centers, grad_fc)


def solution(mesh):
    torus = Mesh(mesh.devices.reshape(4, 4, 4, 2), ("cls_0", "cls_1", "cls_2", "cls_3"))
    placed = (P(CLS, None), P(), P(CLS, None), P())
    return jax.shard_map(
        on_device,
        mesh=torus,
        in_specs=placed,
        out_specs=(P(CLS), P(CLS, None), P(CLS, None)),
        check_vma=False,
    )
```

profile of v0, /device:TPU:1, one launch (start us, length us, event | category | flops | bytes accessed | tf_op | source)
XLA Modules:
  0.0 228.6 jit_solution(8247104401457302656)
XLA Ops:
  0.6 7.2 %fusion.22 = (f32[16]{0:T(128)}, bf16[16,512]{1,0:T(8,128)(2,1)S(1)}) fusion(bf16[16,12544]{1,0:T(8,128)(2,1)} %param.4, bf16[12544,512]{1,0:T(8,128)(2,1)} %param.5), kind=kOutput, calls=%fused_computation.36 | convolution fusion | flops 205553648 | bytes 13262912 | tf_op jit(solution)/shard_map/dot_general | solution.py:95
  7.8 1.1 broadcast_in_dim.52
  8.9 12.0 %all-to-all-start = ((bf16[64,16,512]{2,1,0:T(8,128)(2,1)}), bf16[64,16,512]{2,1,0:T(8,128)(2,1)S(1)}, u32[]{:S(2)}, u32[]{:S(2)}) async-start(bf16[64,16,512]{2,1,0:T(8,128)(2,1)} %broadcast_in_dim.52), calls=%async_computation | async-start | bytes 2097152 | tf_op jit(solution)/shard_map/all_to_all | solution.py:20
  20.9 6.3 %copy.25 = bf16[4096,512]{0,1:T(8,128)(2,1)} copy(bf16[4096,512]{1,0:T(8,128)(2,1)} %param.6) | data formatting | bytes 8388608 | tf_op args[2]
  27.2 3.1 %fusion.7 = f32[4096]{0:T(1024)S(1)} fusion(bf16[4096,512]{0,1:T(8,128)(2,1)} %copy.25), kind=kLoop, calls=%fused_computation.15 | loop fusion | flops 6287360 | bytes 4210688 | tf_op jit(solution)/shard_map/reduce_sum | solution.py:73
  30.3 7.9 %all-to-all-done = bf16[64,16,512]{2,1,0:T(8,128)(2,1)S(1)} async-done(((bf16[64,16,512]{2,1,0:T(8,128)(2,1)}), bf16[64,16,512]{2,1,0:T(8,128)(2,1)S(1)}, u32[]{:S(2)}, u32[]{:S(2)}) %all-to-all-start) | async-done | bytes 1048608 | tf_op jit(solution)/shard_map/all_to_all | solution.py:20
  38.5 7.4 %all_to_all.61 = bf16[2,64,16,512]{3,2,1,0:T(8,128)(2,1)S(1)} all-to-all(bf16[2,64,16,512]{3,2,1,0:T(8,128)(2,1)S(1)} %broadcast_in_dim.53), channel_id=1, replica_groups=mesh['cls_0'=4,'cls_1'=4,'cls_2'=4,'cls_3'=2] {'cls_3'}, dimensions={0} | all-to-all | bytes 4194304 | tf_op jit(solution)/shard_map/all_to_all | solution.py:20
  47.6 1.2 copy-done
  48.8 15.6 %select_reduce_fusion.1 = (f32[2048]{0:T(1024)S(1)}, f32[2048,4096]{1,0:T(8,128)}) fusion(s32[2048]{0:T(1024)S(1)} %broadcast_subtract_fusion, bf16[2048,512]{1,0:T(8,128)(2,1)S(1)} %fusion.8, bf16[4096,512]{0,1:T(8,128)(2,1)S(1)} %copy-done, f32[4096]{0:T(1024)S(1)} %add_rsqrt_fusion), kind=kOutput, calls=%fused_computation.4 | convolution fusion | flops 8621389824 | bytes 39878656 | tf_op jit(solution)/shard_map/dot_general | solution.py:77
  64.3 0.6 multiply_add_fusion
  65.0 18.9 %exponential_reduce_fusion = (f32[2048]{0:T(1024)S(1)}, f32[2048]{0:T(1024)S(1)}) fusion(f32[2048,4096]{1,0:T(8,128)} %get-tuple-element.25, f32[2048]{0:T(1024)S(1)} %get-tuple-element.23, s32[2048]{0:T(1024)S(1)} %broadcast_subtract_fusion), kind=kLoop, calls=%fused_computation.2 | loop fusion | flops 58716160 | bytes 33587200 | tf_op jit(solution)/shard_map/reduce_sum | solution.py:109
  83.9 8.0 %all_to_all.62 = f32[8,1,4096]{2,1,0:T(1,128)S(1)} all-to-all(f32[8,1,4096]{2,1,0:T(1,128)S(1)} %broadcast_in_dim.56), channel_id=1, replica_groups=mesh['cls_0'=4,'cls_1'=4,'cls_2'=4,'cls_3'=2] {'cls_2','cls_3'}, dimensions={0} | all-to-all | bytes 262144 | tf_op jit(solution)/shard_map/all_to_all | solution.py:20
  92.2 10.1 %all_to_all.63 = f32[16,1,4096]{2,1,0:T(1,128)S(1)} all-to-all(f32[16,1,4096]{2,1,0:T(1,128)S(1)} %broadcast_in_dim.57), channel_id=1, replica_groups=mesh['cls_0'=4,'cls_1'=4,'cls_2'=4,'cls_3'=2] {'cls_0','cls_1'}, dimensions={0} | all-to-all | bytes 524288 | tf_op jit(solution)/shard_map/all_to_all | solution.py:20
  103.1 20.8 %multiply_convert_fusion = bf16[2048,4096]{1,0:T(8,128)(2,1)S(1)} fusion(f32[2048,4096]{1,0:T(8,128)} %get-tuple-element.25, f32[2048]{0:T(1024)} %get-tuple-element.22, f32[2048]{0:T(1024)S(1)} %get-tuple-element.20, f32[2048]{0:T(1024)S(1)} %get-tuple-element.23, s32[2048]{0:T(1024)S(1)} %broadcast_subtract_fusion), kind=kLoop, calls=%fused_computation | loop fusion | flops 83886080 | bytes 50364416 | tf_op jit(solution)/shard_map/convert_element_type | solution.py:119
  124.0 11.7 %fusion.13 = bf16[2048,512]{1,0:T(8,128)(2,1)} fusion(bf16[2048,4096]{1,0:T(8,128)(2,1)S(1)} %multiply_convert_fusion, bf16[4096,512]{0,1:T(8,128)(2,1)S(1)} %copy-done.1, f32[4096]{0:T(1024)} %copy-done.5), kind=kOutput, calls=%fused_computation.21 | convolution fusion | flops 8597274624 | bytes 23085056 | tf_op jit(solution)/shard_map/dot_general | solution.py:128
  135.7 1.8 copy.40
  137.5 7.3 %all_to_all.64 = bf16[2,64,16,512]{3,2,1,0:T(8,128)(2,1)S(1)} all-to-all(bf16[2,64,16,512]{3,2,1,0:T(8,128)(2,1)S(1)} %bitcast.29), channel_id=1, replica_groups=mesh['cls_0'=4,'cls_1'=4,'cls_2'=4,'cls_3'=2] {'cls_3'}, dimensions={0} | all-to-all | bytes 4194304 | tf_op jit(solution)/shard_map/all_to_all | solution.py:60
  144.8 1.7 reduce_sum.119
  146.5 4.7 %all-to-all-start.5 = ((bf16[64,16,512]{2,1,0:T(8,128)(2,1)}), bf16[64,16,512]{2,1,0:T(8,128)(2,1)S(1)}, u32[]{:S(2)}, u32[]{:S(2)}) async-start(bf16[64,16,512]{2,1,0:T(8,128)(2,1)} %reduce_sum.119), calls=%async_computation.5 | async-start | bytes 2097152 | tf_op jit(solution)/shard_map/all_to_all | solution.py:68
  151.2 1.9 all_to_all.48
  153.2 1.1 copy.30
  154.3 14.7 %all-to-all-done.5 = bf16[64,16,512]{2,1,0:T(8,128)(2,1)S(1)} async-done(((bf16[64,16,512]{2,1,0:T(8,128)(2,1)}), bf16[64,16,512]{2,1,0:T(8,128)(2,1)S(1)}, u32[]{:S(2)}, u32[]{:S(2)}) %all-to-all-start.5) | async-done | bytes 1048608 | tf_op jit(solution)/shard_map/all_to_all | solution.py:68
  169.5 1.2 broadcast_in_dim.60
  170.7 5.0 %all-to-all-start.6 = ((bf16[64,16,512]{2,1,0:T(8,128)(2,1)}), bf16[64,16,512]{2,1,0:T(8,128)(2,1)S(1)}, u32[]{:S(2)}, u32[]{:S(2)}) async-start(bf16[64,16,512]{2,1,0:T(8,128)(2,1)} %broadcast_in_dim.60), calls=%async_computation.6 | async-start | bytes 2097152 | tf_op jit(solution)/shard_map/all_to_all | solution.py:20
  175.7 16.3 %fusion.3 = (f32[4096]{0:T(1024)S(1)}, f32[4096,512]{0,1:T(8,128)}) fusion(bf16[4096,512]{0,1:T(8,128)(2,1)} %copy.25, f32[4096]{0:T(1024)S(1)} %copy-done.6, bf16[2048,4096]{1,0:T(8,128)(2,1)} %copy-done.2, bf16[2048,512]{1,0:T(8,128)(2,1)} %copy-done.4), kind=kOutput, calls=%fused_computation.11 | convolution fusion | flops 8598319104 | bytes 31490048 | tf_op jit(solution)/shard_map/dot_general | solution.py:120
  192.6 8.2 %all_to_all.65 = bf16[2,64,16,512]{3,2,1,0:T(8,128)(2,1)S(1)} all-to-all(bf16[2,64,16,512]{3,2,1,0:T(8,128)(2,1)S(1)} %broadcast_in_dim.61), channel_id=1, replica_groups=mesh['cls_0'=4,'cls_1'=4,'cls_2'=4,'cls_3'=2] {'cls_3'}, dimensions={0} | all-to-all | bytes 4194304 | tf_op jit(solution)/shard_map/all_to_all | solution.py:20
  200.7 7.6 %all-to-all-start.8 = ((bf16[16,128,98]{2,0,1:T(8,128)(2,1)}), bf16[16,128,98]{2,0,1:T(8,128)(2,1)S(1)}, u32[]{:S(2)}, u32[]{:S(2)}) async-start(bf16[16,128,98]{2,0,1:T(8,128)(2,1)} %copy.30), calls=%async_computation.8 | async-start | bytes 1048576 | tf_op jit(solution)/shard_map/all_to_all | solution.py:94
  208.3 8.2 %fusion.6 = bf16[4096,512]{0,1:T(8,128)(2,1)} fusion(f32[4096,512]{0,1:T(8,128)} %get-tuple-element.27, bf16[4096,512]{0,1:T(8,128)(2,1)} %copy.25, f32[4096]{0:T(1024)S(1)} %get-tuple-element.26, f32[4096]{0:T(1024)S(1)} %copy-done.6), kind=kLoop, calls=%fused_computation.14 | loop fusion | flops 12582912 | bytes 16809984 | tf_op jit(solution)/shard_map/convert_element_type | solution.py:126
  216.6 6.4 %copy.31 = bf16[4096,512]{1,0:T(8,128)(2,1)} copy(bf16[4096,512]{0,1:T(8,128)(2,1)} %fusion.6) | data formatting | bytes 8388608
  223.0 1.2 dynamic-slice_subtract_fusion
  224.2 1.6 copy.29
  225.8 2.7 %convolution_bitcast_fusion = f32[98,512]{1,0:T(8,128)} fusion(bf16[2048,512]{1,0:T(8,128)(2,1)} %bitcast.28, bf16[2048,98]{1,0:T(8,128)(2,1)S(1)} %bitcast.31), kind=kOutput, calls=%fused_computation.25 | convolution fusion | flops 205520896 | bytes 2699264 | tf_op jit(solution)/shard_map/dot_general | solution.py:136
  (38 shorter events, 4.1 us)
Async XLA Ops:
  7.8 19.4 %copy-start.7 = (s32[2048]{0:T(1024)S(1)}, s32[2048]{0:T(1024)}, u32[]{:S(2)}) copy-start(s32[2048]{0:T(1024)} %param.7) | copy-start | bytes 24580
  8.9 29.3 %all-to-all-start = ((bf16[64,16,512]{2,1,0:T(8,128)(2,1)}), bf16[64,16,512]{2,1,0:T(8,128)(2,1)S(1)}, u32[]{:S(2)}, u32[]{:S(2)}) async-start(bf16[64,16,512]{2,1,0:T(8,128)(2,1)} %broadcast_in_dim.52), calls=%async_computation | async-start | bytes 2097152 | tf_op jit(solution)/shard_map/all_to_all | solution.py:20
  30.3 17.2 %copy-start.5 = (f32[4096]{0:T(1024)}, f32[4096]{0:T(1024)S(1)}, u32[]{:S(2)}) copy-start(f32[4096]{0:T(1024)S(1)} %add_rsqrt_fusion) | copy-start | bytes 49156
  46.6 2.2 copy-start
  48.8 15.6 %copy-start.4 = (bf16[2048,512]{1,0:T(8,128)(2,1)}, bf16[2048,512]{1,0:T(8,128)(2,1)S(1)}, u32[]{:S(2)}) copy-start(bf16[2048,512]{1,0:T(8,128)(2,1)S(1)} %fusion.8) | copy-start | bytes 6291460
  103.1 20.8 %copy-start.1 = (bf16[4096,512]{0,1:T(8,128)(2,1)S(1)}, bf16[4096,512]{0,1:T(8,128)(2,1)}, u32[]{:S(2)}) copy-start(bf16[4096,512]{0,1:T(8,128)(2,1)} %copy.25) | copy-start | bytes 12582916
  124.0 11.7 %copy-start.2 = (bf16[2048,4096]{1,0:T(8,128)(2,1)}, bf16[2048,4096]{1,0:T(8,128)(2,1)S(1)}, u32[]{:S(2)}) copy-start(bf16[2048,4096]{1,0:T(8,128)(2,1)S(1)} %multiply_convert_fusion) | copy-start | bytes 50331652
  135.7 18.6 %copy-start.8 = (f32[16]{0:T(128)S(1)}, f32[16]{0:T(128)}, u32[]{:S(2)}) copy-start(f32[16]{0:T(128)} %get-tuple-element.28) | copy-start | bytes 196
  135.7 15.5 %copy-start.3 = (bf16[16,12544]{1,0:T(8,128)(2,1)S(1)}, bf16[16,12544]{1,0:T(8,128)(2,1)}, u32[]{:S(2)}) copy-start(bf16[16,12544]{1,0:T(8,128)(2,1)} %param.4) | copy-start | bytes 1204228
  137.5 38.2 %copy-start.6 = (f32[4096]{0:T(1024)S(1)}, f32[4096]{0:T(1024)}, u32[]{:S(2)}) copy-start(f32[4096]{0:T(1024)} %copy-done.5) | copy-start | bytes 49156
  146.5 22.5 %all-to-all-start.5 = ((bf16[64,16,512]{2,1,0:T(8,128)(2,1)}), bf16[64,16,512]{2,1,0:T(8,128)(2,1)S(1)}, u32[]{:S(2)}, u32[]{:S(2)}) async-start(bf16[64,16,512]{2,1,0:T(8,128)(2,1)} %reduce_sum.119), calls=%async_computation.5 | async-start | bytes 2097152 | tf_op jit(solution)/shard_map/all_to_all | solution.py:68
  170.7 21.6 %all-to-all-start.6 = ((bf16[64,16,512]{2,1,0:T(8,128)(2,1)}), bf16[64,16,512]{2,1,0:T(8,128)(2,1)S(1)}, u32[]{:S(2)}, u32[]{:S(2)}) async-start(bf16[64,16,512]{2,1,0:T(8,128)(2,1)} %broadcast_in_dim.60), calls=%async_computation.6 | async-start | bytes 2097152 | tf_op jit(solution)/shard_map/all_to_all | solution.py:20
  200.7 25.1 %all-to-all-start.8 = ((bf16[16,128,98]{2,0,1:T(8,128)(2,1)}), bf16[16,128,98]{2,0,1:T(8,128)(2,1)S(1)}, u32[]{:S(2)}, u32[]{:S(2)}) async-start(bf16[16,128,98]{2,0,1:T(8,128)(2,1)} %copy.30), calls=%async_computation.8 | async-start | bytes 1048576 | tf_op jit(solution)/shard_map/all_to_all | solution.py:94
where the time goes:
time: 230 us; the launch traced here: 229 us
  other arithmetic  57.3 us (25%)
  matrix products  53.5 us (23%)
  blocking collectives  41 us (18%)
  starting transfers between devices  29.2 us (13%)
  local copies, waits for them, and re-layouts  23.8 us (10%)
  waiting for transfers between devices  22.8 us (10%)
    all_to_all x4, blocking collectives, from_everyone(): return lax.all_to_all(copies, axis, split_axis=0, concat_axis=0, tiled=True)  33.7 us
    convert_element_type x1, other arithmetic, on_device(): grad_cos = (logit_scale * (probs - is_target.astype(jnp.float32)) * jnp.w...  20.8 us
    reduce_sum x1, other arithmetic, on_device(): jnp.sum(jnp.exp(logits - logit_scale), axis=1)  18.9 us
    all_to_all x2, starting transfers between devices, from_everyone(): return lax.all_to_all(copies, axis, split_axis=0, concat_axis=0, tiled=True)  17 us
    dot_general x1, matrix products, on_device(): lax.dot_general(grad_cos, emb_low, (((0,), (0,)), ((), ())), preferred_el...  16.3 us
    dot_general x1, matrix products, margin_logits(): lax.dot_general(emb_low, center_low, (((1,), (1,)), ((), ())), preferred_...  15.6 us
    all_to_all x1, waiting for transfers between devices, sum_by_axis(): lax.all_to_all(own.astype(jnp.bfloat16), far, 0, 0, tiled=True)  14.7 us
    unnamed x20, local copies, waits for them, and re-layouts  14 us
  transfers between devices with their start and end apart: 4, of which 3 were waited for; matrix products, arithmetic and copies ran while one was open for 19% of the time, Pallas kernels for 0%

commit v1 on v0

v1 whole, which is shorter than its diff:
```python
import functools
import math

import jax
import jax.numpy as jnp
from jax import lax
from jax.experimental import pallas as pl
from jax.experimental.pallas import tpu as pltpu
from jax.sharding import Mesh
from jax.sharding import PartitionSpec as P

CLS = ("cls_0", "cls_1", "cls_2", "cls_3")
MESH = pl.DeviceIdType.MESH

logit_scale = 64.0
cos_margin = math.cos(0.5)
sin_margin = math.sin(0.5)
epsilon = 1e-06
exp2_scale = logit_scale / math.log(2.0)

N = 128
D = 512
F = 12544
F_DEV = F // N
OWN = 16
CLASSES = 4096
BT = 512
W_CHUNK = 1792
N_W = F // W_CHUNK
JA = 1024
JB = 1024
JC = 512

ORDERS = ((0, 1, 2), (1, 2, 0), (2, 0, 1), (0, 2, 1))

f32 = jnp.float32
bf16 = jnp.bfloat16


def last_dims(a, b):
    return lax.dot_general(a, b, (((1,), (1,)), ((), ())), preferred_element_type=f32)


def plain_dot(a, b):
    return lax.dot_general(a, b, (((1,), (0,)), ((), ())), preferred_element_type=f32)


def eye(n):
    r = lax.broadcasted_iota(jnp.int32, (n, n), 0)
    c = lax.broadcasted_iota(jnp.int32, (n, n), 1)
    return (r == c).astype(f32).astype(bf16)


def kernel(
    feat, w_hbm, centers_hbm, labels,
    loss_out, fc_out, gc_hbm,
    E, cen, clow, ct, tt, emb, gemb, gt, G, rb0, gs, rb1, gs2, rb2, gs3, rb3, cols,
    own_emb, ar_send, ar_recv, rows,
    w_sem, c_sem, out_sem, ag_send, ag_recv, d_send, d_recv, rs_send, rs_recv,
    s_send, s_recv, a_send, a_recv,
):
    me = tuple(lax.axis_index(name) for name in CLS)
    core = me[3]
    idx = ((me[0] * 4 + me[1]) * 4 + me[2]) * 2 + core
    offset = idx * CLASSES
    place = core * (N // 2) + idx // 2

    def peer(axis, k):
        size = 2 if axis == 3 else 4
        coords = list(me)
        coords[axis] = lax.rem(me[axis] + k, size)
        return tuple(coords)

    def w_copy(i):
        return pltpu.make_async_copy(
            w_hbm.at[pl.ds(i * W_CHUNK, W_CHUNK)],
            E.at[i // 2, pl.ds((i % 2) * 2048, W_CHUNK)],
            w_sem.at[i],
        )

    c_copy = pltpu.make_async_copy(centers_hbm, cen, c_sem)
    for i in range(N_W):
        w_copy(i).start()
    c_copy.start()

    barrier = pltpu.get_barrier_semaphore()
    for axis in range(3):
        for k in (1, 2, 3):
            pl.semaphore_signal(barrier, inc=1, device_id=peer(axis, k), device_id_type=MESH)
    pl.semaphore_signal(barrier, inc=1, device_id=peer(3, 1), device_id_type=MESH)

    acc = jnp.zeros((OWN, D), f32)
    for i in range(N_W):
        w_copy(i).wait()
        acc = acc + plain_dot(
            feat[:, i * W_CHUNK : (i + 1) * W_CHUNK], E[i // 2, (i % 2) * 2048 : (i % 2) * 2048 + W_CHUNK]
        )
    own = acc.astype(bf16).astype(f32)
    own_inv = lax.rsqrt(jnp.sum(own * own, axis=1, keepdims=True) + epsilon)
    own_emb[...] = own
    own_low = (own * own_inv).astype(bf16)

    def put_own(buf, value):
        for p in range(4):
            buf[p, core, me[0], me[1], me[2]] = value[:, p * 128 : (p + 1) * 128]

    def view(buf, p, gathered, at=None):
        at = me if at is None else at
        where = tuple(slice(None) if a in gathered else at[a] for a in range(3))
        return buf.at[(p, core) + where]

    def ag_copy(buf, inst, p, s, k):
        order = ORDERS[p]
        v = view(buf, p, order[:s])
        return pltpu.make_async_remote_copy(
            src_ref=v, dst_ref=v,
            send_sem=ag_send.at[inst, p, s, k - 1], recv_sem=ag_recv.at[inst, p, s, k - 1],
            device_id=peer(order[s], k), device_id_type=MESH,
        )

    def ag_start(buf, inst, s):
        for k in (1, 2, 3):
            for p in range(4):
                ag_copy(buf, inst, p, s, k).start()

    def ag_wait(buf, inst, s):
        for k in (1, 2, 3):
            for p in range(4):
                ag_copy(buf, inst, p, s, k).wait_recv()

    def ag_drain(buf, inst):
        for s in range(3):
            for k in (1, 2, 3):
                for p in range(4):
                    ag_copy(buf, inst, p, s, k).wait_send()

    def pair_copy(buf, inst, p):
        v = buf.at[p, core]
        return pltpu.make_async_remote_copy(
            src_ref=v, dst_ref=v,
            send_sem=d_send.at[inst, p], recv_sem=d_recv.at[inst, p],
            device_id=peer(3, 1), device_id_type=MESH,
        )

    def pair_start(buf, inst):
        for p in range(4):
            pair_copy(buf, inst, p).start()

    def pair_wait(buf, inst):
        for p in range(4):
            pair_copy(buf, inst, p).wait()

    def block(buf, bt):
        c, y0 = bt // 2, (bt % 2) * 2
        return jnp.concatenate([buf[p, c, pl.ds(y0, 2)].reshape(BT, 128) for p in range(4)], axis=1)

    put_own(emb, own_low)
    pl.semaphore_wait(barrier, 10)
    ag_start(emb, 0, 0)

    c_copy.wait()

    @pl.loop(0, CLASSES // JC)
    def _(i):
        r = pl.ds(pl.multiple_of(i * JC, JC), JC)
        cf = cen[r, :].astype(f32)
        inv = lax.rsqrt(jnp.sum(cf * cf, axis=1, keepdims=True) + epsilon)
        low = (cf * inv).astype(bf16)
        clow[r, :] = low
        ct[:, r] = last_dims(eye(D), low).astype(bf16)

    ag_wait(emb, 0, 0)
    ag_start(emb, 0, 1)

    def target_rows(bt):
        lab = labels[pl.ds(bt, 1), :] - offset
        gt[bt] = jnp.zeros((D, BT), f32)

        @pl.loop(0, CLASSES // JB)
        def _(j):
            j0 = pl.multiple_of(j * JB, JB)
            hot = (lab - j0) == lax.broadcasted_iota(jnp.int32, (JB, BT), 0)
            hot = jnp.where(hot, 1.0, 0.0).astype(bf16)
            gt[bt] += plain_dot(ct[:, pl.ds(j0, JB)], hot)

        tt[bt] = gt[bt].astype(bf16)

    @pl.loop(0, 4)
    def _(bt):
        target_rows(bt)

        @pl.when(bt == 0)
        def _():
            ag_wait(emb, 0, 1)
            ag_start(emb, 0, 2)

    ag_wait(emb, 0, 2)
    pair_start(emb, 0)
    pair_wait(emb, 0)

    def tile_of(dev):
        return jnp.minimum((dev * F_DEV) // 128, F // 128 - 2)

    def feature_copy(dev):
        coords = (dev // 32, lax.rem(dev // 8, 4), lax.rem(dev // 2, 4), lax.rem(dev, 2))
        return pltpu.make_async_remote_copy(
            src_ref=feat.at[:, pl.ds(pl.multiple_of(tile_of(dev) * 128, 128), 256)],
            dst_ref=cols.at[place],
            send_sem=a_send, recv_sem=a_recv, device_id=coords, device_id_type=MESH,
        )

    cols[place] = feat[:, pl.ds(pl.multiple_of(tile_of(idx) * 128, 128), 256)]

    @pl.loop(1, N)
    def _(k):
        feature_copy(lax.rem(idx + k, N)).start()

    rows[...] = jnp.zeros_like(rows)

    @pl.loop(0, 4 * (CLASSES // JA))
    def _(i):
        bt, j0 = i // (CLASSES // JA), pl.multiple_of(lax.rem(i, CLASSES // JA) * JA, JA)
        cosines = last_dims(clow[pl.ds(j0, JA), :], block(emb, bt))
        lab = labels[pl.ds(bt, 1), :] - offset - j0
        hot = lab == lax.broadcasted_iota(jnp.int32, (JA, BT), 0)
        e = jnp.where(hot, 0.0, jnp.exp2(cosines * exp2_scale))
        rows[bt] += jnp.sum(e.reshape(JA // 8, 8, BT), axis=0)
        E[bt, pl.ds(j0, JA), :] = e.astype(bf16)

    target = []
    for bt in range(4):
        lab = labels[bt : bt + 1, :] - offset
        here = jnp.logical_and(lab >= 0, lab < CLASSES)
        emb_t = last_dims(eye(D), block(emb, bt))
        tc = jnp.sum(emb_t * tt[bt].astype(f32), axis=0, keepdims=True)
        ts = jnp.sqrt(1.0 - tc * tc)
        margined = logit_scale * (tc * cos_margin - ts * sin_margin)
        slope = cos_margin + sin_margin * tc / ts
        e_t = jnp.where(here, jnp.exp(margined), 0.0)
        slope = jnp.where(here, slope, 0.0)
        target.append((e_t, slope))
        ar_send[0, bt : bt + 1, :] = jnp.sum(rows[bt], axis=0, keepdims=True) + e_t
        ar_send[0, 4 + bt : 5 + bt, :] = jnp.where(here, margined, 0.0)

    AR_AXES = (3, 2, 1, 0)

    def ar_copy(s, k):
        return pltpu.make_async_remote_copy(
            src_ref=ar_send.at[s], dst_ref=ar_recv.at[s, k - 1],
            send_sem=s_send.at[s, k - 1], recv_sem=s_recv.at[s, k - 1],
            device_id=peer(AR_AXES[s], k), device_id_type=MESH,
        )

    def ar_peers(s):
        return (1,) if s == 0 else (1, 2, 3)

    def ar_start(s):
        for k in ar_peers(s):
            ar_copy(s, k).start()

    def ar_finish(s):
        total = ar_send[s]
        for k in ar_peers(s):
            ar_copy(s, k).wait_recv()
            total = total + ar_recv[s, k - 1]
        ar_send[s + 1] = total

    ar_start(0)

    @pl.loop(0, 4)
    def _(bt):
        gt[bt] = jnp.zeros((D, BT), f32)

        @pl.loop(0, CLASSES // JB)
        def _(j):
            j0 = pl.multiple_of(j * JB, JB)
            gt[bt] += plain_dot(ct[:, pl.ds(j0, JB)], E[bt, pl.ds(j0, JB), :])

        for s in range(4):
            @pl.when(bt == s)
            def _():
                ar_finish(s)
                if s < 3:
                    ar_start(s + 1)

    for s in range(4):
        for k in ar_peers(s):
            ar_copy(s, k).wait_send()

    for bt in range(4):
        total = ar_send[4, bt : bt + 1, :]
        loss_out[bt : bt + 1, :] = jnp.log(total) - ar_send[4, 4 + bt : 5 + bt, :]
        e_t, slope = target[bt]
        scale = logit_scale / total
        v = (e_t - total) * slope * scale
        rows[bt, 0:1, :] = scale
        rows[bt, 1:2, :] = v
        g = (gt[bt] * scale + v * tt[bt].astype(f32)).astype(bf16)
        back = last_dims(eye(BT), g).astype(bf16)
        for p in range(4):
            G[p, bt // 2, (bt % 2) * 2 : (bt % 2) * 2 + 2] = back[:, p * 128 : (p + 1) * 128].reshape(2, 4, 4, OWN, 128)

    def rs0_copy(p):
        return pltpu.make_async_remote_copy(
            src_ref=G.at[p, 1 - core], dst_ref=rb0.at[p],
            send_sem=d_send.at[2, p], recv_sem=d_recv.at[2, p],
            device_id=peer(3, 1), device_id_type=MESH,
        )

    def rs_copy(s, p, k):
        order = ORDERS[p]
        axis = order[2 - s]
        to = peer(axis, k)
        if s == 0:
            src = gs.at[(p,) + tuple(to[a] if a == axis else slice(None) for a in range(3))]
            dst = rb1.at[p, k - 1]
        elif s == 1:
            left = sorted(order[:2])
            src = gs2.at[(p,) + tuple(to[a] if a == axis else slice(None) for a in left)]
            dst = rb2.at[p, k - 1]
        else:
            src = gs3.at[p, to[axis]]
            dst = rb3.at[p, k - 1]
        return pltpu.make_async_remote_copy(
            src_ref=src, dst_ref=dst,
            send_sem=rs_send.at[s, p, k - 1], recv_sem=rs_recv.at[s, p, k - 1],
            device_id=to, device_id_type=MESH,
        )

    def rs_start(s):
        for k in (1, 2, 3):
            for p in range(4):
                rs_copy(s, p, k).start()

    def rs_step(stage):
        if stage == 0:
            for p in range(4):
                rs0_copy(p).wait()
                gs[p] = (G[p, core].astype(f32) + rb0[p].astype(f32)).astype(bf16)
            rs_start(0)
            return None
        s = stage - 1
        out = []
        for p in range(4):
            order = ORDERS[p]
            axis = order[2 - s]
            if s == 0:
                total = gs[(p,) + tuple(me[a] if a == axis else slice(None) for a in range(3))]
                bufs = rb1
            elif s == 1:
                total = gs2[(p,) + tuple(me[a] if a == axis else slice(None) for a in sorted(order[:2]))]
                bufs = rb2
            else:
                total = gs3[p, me[axis]]
                bufs = rb3
            total = total.astype(f32)
            for k in (1, 2, 3):
                rs_copy(s, p, k).wait_recv()
                total = total + bufs[p, k - 1].astype(f32)
            if s == 0:
                gs2[p] = total.astype(bf16)
            elif s == 1:
                gs3[p] = total.astype(bf16)
            else:
                out.append(total)
        if s < 2:
            rs_start(s + 1)
            return None
        for s in range(3):
            for p in range(4):
                for k in (1, 2, 3):
                    rs_copy(s, p, k).wait_send()
        return jnp.concatenate(out, axis=1)

    def owner_step():
        grad_dir = rs_step(3)
        own = own_emb[...]
        inv = lax.rsqrt(jnp.sum(own * own, axis=1, keepdims=True) + epsilon)
        direction = own * inv
        along = jnp.sum(grad_dir * direction, axis=1, keepdims=True)
        put_own(gemb, ((grad_dir - direction * along) * inv).astype(bf16))
        ag_start(gemb, 1, 0)

    def ag_step(s):
        ag_wait(gemb, 1, s)
        if s < 2:
            ag_start(gemb, 1, s + 1)
        else:
            pair_start(gemb, 1)

    for p in range(4):
        rs0_copy(p).start()

    def out_copy(i):
        r = pl.ds(pl.multiple_of(i * JC, JC), JC)
        return pltpu.make_async_copy(cen.at[r], gc_hbm.at[r], out_sem.at[i])

    steps = {
        0: functools.partial(rs_step, 0),
        2: functools.partial(rs_step, 1),
        4: functools.partial(rs_step, 2),
        5: owner_step,
        6: functools.partial(ag_step, 0),
        7: functools.partial(ag_step, 1),
    }

    @pl.loop(0, CLASSES // JC)
    def _(i):
        j0 = pl.multiple_of(i * JC, JC)
        r = pl.ds(j0, JC)
        gu = jnp.zeros((JC, D), f32)
        for bt in range(4):
            lab = labels[bt : bt + 1, :] - offset - j0
            hot = lab == lax.broadcasted_iota(jnp.int32, (JC, BT), 0)
            scaled = E[bt, r, :].astype(f32) * rows[bt, 0:1, :]
            gc = jnp.where(hot, rows[bt, 1:2, :], scaled).astype(bf16)
            gu = gu + plain_dot(gc, block(emb, bt))
        cf = cen[r, :].astype(f32)
        inv = lax.rsqrt(jnp.sum(cf * cf, axis=1, keepdims=True) + epsilon)
        cdir = cf * inv
        along = jnp.sum(gu * cdir, axis=1, keepdims=True)
        cen[r, :] = ((gu - cdir * along) * inv).astype(bf16)
        out_copy(i).start()
        for at, step in steps.items():
            @pl.when(i == at)
            def _():
                step()

    ag_step(2)

    others = cols.at[pl.ds(0, N - 1)]
    pltpu.make_async_copy(others, others, a_send).wait()
    pltpu.make_async_copy(others, others, a_recv).wait()

    start = idx * F_DEV - tile_of(idx) * 128
    pick = lax.broadcasted_iota(jnp.int32, (104, 256), 1) == lax.broadcasted_iota(jnp.int32, (104, 256), 0) + start
    pick = pick.astype(f32).astype(bf16)
    mine = [
        last_dims(pick, cols[bt * 32 : (bt + 1) * 32].reshape(BT, 256)).astype(bf16) for bt in range(4)
    ]
    pair_wait(gemb, 1)
    fc = jnp.zeros((104, D), f32)
    for bt in range(4):
        fc = fc + plain_dot(mine[bt], block(gemb, bt))
    fc_out[...] = fc[0:F_DEV]

    for i in range(CLASSES // JC):
        out_copy(i).wait()
    ag_drain(emb, 0)
    ag_drain(gemb, 1)


def on_device(features, fc_weight, centers, labels):
    ordered = labels.reshape(64, 2, OWN).transpose(1, 0, 2).reshape(4, BT)
    vmem = pl.BlockSpec(memory_space=pltpu.VMEM)
    anywhere = pl.BlockSpec(memory_space=pl.ANY)
    dma = pltpu.SemaphoreType.DMA
    loss_all, grad_fc, grad_centers = pl.pallas_call(
        kernel,
        out_shape=(
            jax.ShapeDtypeStruct((4, BT), f32),
            jax.ShapeDtypeStruct((F_DEV, D), f32),
            jax.ShapeDtypeStruct((CLASSES, D), bf16),
        ),
        in_specs=[vmem, anywhere, anywhere, vmem],
        out_specs=(vmem, vmem, anywhere),
        scratch_shapes=[
            pltpu.VMEM((4, CLASSES, BT), bf16),
            pltpu.VMEM((CLASSES, D), bf16),
            pltpu.VMEM((CLASSES, D), bf16),
            pltpu.VMEM((D, CLASSES), bf16),
            pltpu.VMEM((4, D, BT), bf16),
            pltpu.VMEM((4, 2, 4, 4, 4, OWN, 128), bf16),
            pltpu.VMEM((4, 2, 4, 4, 4, OWN, 128), bf16),
            pltpu.VMEM((4, D, BT), f32),
            pltpu.VMEM((4, 2, 4, 4, 4, OWN, 128), bf16),
            pltpu.VMEM((4, 4, 4, 4, OWN, 128), bf16),
            pltpu.VMEM((4, 4, 4, 4, OWN, 128), bf16),
            pltpu.VMEM((4, 3, 4, 4, OWN, 128), bf16),
            pltpu.VMEM((4, 4, 4, OWN, 128), bf16),
            pltpu.VMEM((4, 3, 4, OWN, 128), bf16),
            pltpu.VMEM((4, 4, OWN, 128), bf16),
            pltpu.VMEM((4, 3, OWN, 128), bf16),
            pltpu.VMEM((N, OWN, 256), bf16),
            pltpu.VMEM((OWN, D), f32),
            pltpu.VMEM((5, 8, BT), f32),
            pltpu.VMEM((4, 3, 8, BT), f32),
            pltpu.VMEM((4, 8, BT), f32),
            dma((N_W,)),
            dma,
            dma((CLASSES // JC,)),
            dma((2, 4, 3, 3)),
            dma((2, 4, 3, 3)),
            dma((3, 4)),
            dma((3, 4)),
            dma((3, 4, 3)),
            dma((3, 4, 3)),
            dma((4, 3)),
            dma((4, 3)),
            dma,
            dma,
        ],
        compiler_params=pltpu.CompilerParams(
            collective_id=0, has_side_effects=True, vmem_limit_bytes=66_000_000
        ),
    )(features, fc_weight, centers, ordered)
    position = (lax.axis_index("cls_3") * 64 + lax.axis_index(CLS[:3])) * OWN
    loss = lax.dynamic_slice_in_dim(loss_all.reshape(-1), position, OWN)
    return (loss, grad_centers, grad_fc)


def solution(mesh):
    torus = Mesh(mesh.devices.reshape(4, 4, 4, 2), CLS)
    placed = (P(CLS, None), P(), P(CLS, None), P())
    return jax.shard_map(
        on_device,
        mesh=torus,
        in_specs=placed,
        out_specs=(P(CLS), P(CLS, None), P(CLS, None)),
        check_vma=False,
    )
```

time: 230 us -> 116 us (0.50)
  Pallas kernels: 0 us -> 107 us
  other arithmetic: 57.3 us -> 0 us
  matrix products: 53.5 us -> 0 us
  blocking collectives: 41 us -> 0 us
  starting transfers between devices: 29.2 us -> 0 us
  waiting for transfers between devices: 22.8 us -> 0 us
  local copies, waits for them, and re-layouts: 23.8 us -> 8.01 us
    pallas_call x0 -> x1, Pallas kernels: none -> 107 us  [on_device(): pl.pallas_call(kernel, out_shape=(jax.ShapeDtypeStruct((4, BT), f32), jax...]
    dot_general x5 -> x0, matrix products: 53.5 us -> none  [the longest x1 16.3 us: on_device(): lax.dot_general(grad_cos, emb_low, (((0,), (0,)), ((), ())), preferred_el...]
    all_to_all x5 -> x0, blocking collectives: 41 us -> none  [the longest x4 33.7 us: from_everyone(): return lax.all_to_all(copies, axis, split_axis=0, concat_axis=0, tiled=True)]
    convert_element_type x5 -> x0, other arithmetic: 30.1 us -> none  [the longest x1 20.8 us: on_device(): grad_cos = (logit_scale * (probs - is_target.astype(jnp.float32)) * jnp.w...]
    all_to_all x4 -> x0, starting transfers between devices: 29.2 us -> none  [the longest x2 17 us: from_everyone(): return lax.all_to_all(copies, axis, split_axis=0, concat_axis=0, tiled=True)]
    reduce_sum x8 -> x0, other arithmetic: 24.8 us -> none  [the longest x1 18.9 us: on_device(): jnp.sum(jnp.exp(logits - logit_scale), axis=1)]
    all_to_all x4 -> x0, waiting for transfers between devices: 22.8 us -> none  [the longest x1 14.7 us: sum_by_axis(): lax.all_to_all(own.astype(jnp.bfloat16), far, 0, 0, tiled=True)]
    unnamed x20 -> x5, local copies, waits for them, and re-layouts: 14 us -> 5.9 us
  transfers between devices with their start and end apart: 4 -> 0, of which waited for: 3 -> 0; matrix products, arithmetic and copies ran while one was open for 19% -> 0% of each run, Pallas kernels for 0% -> 0%
where the time goes in v1:
time: 116 us
  Pallas kernels  107 us (92%)
  local copies, waits for them, and re-layouts  8.01 us (7%)
    pallas_call x1, Pallas kernels, on_device(): pl.pallas_call(kernel, out_shape=(jax.ShapeDtypeStruct((4, BT), f32), jax...  107 us
    unnamed x5, local copies, waits for them, and re-layouts  5.9 us

profile of v1, /device:TPU:1, one launch (start us, length us, event | category | flops | bytes accessed | tf_op | source)
XLA Modules:
  0.0 116.1 jit_solution(16405575826357532688)
XLA Ops:
  0.6 0.8 reshape.15
  1.5 0.7 reshape.16.labels
  2.2 107.4 %shard_map.67 = (f32[4,512]{1,0:T(4,128)}, f32[98,512]{1,0:T(8,128)}, bf16[4096,512]{1,0:T(8,128)(2,1)}) custom-call(bf16[16,12544]{1,0:T(8,128)(2,1)} %feat.1, bf16[12544,512]{1,0:T(8,128)(2,1)} %w_hbm.1, bf16[4096,512]{1,0:T(8,128)(2,1)} %centers_hbm.1, s32[4,512]{1,0:T(4,128)} %reshape.16.labels), custom_call_target="tpu_custom_call" | custom-call | tf_op jit(solution)/shard_map/pallas_call | solution.py:458
  109.6 0.7 copy.8
  110.3 0.6 dynamic_slice.3
  110.9 0.0 copy-start
  110.9 4.5 %copy.11 = bf16[4096,512]{1,0:T(8,128)(2,1)} copy(bf16[4096,512]{1,0:T(8,128)(2,1)} %get-tuple-element.13) | data formatting | bytes 8388608
  115.4 0.0 copy-done
  115.4 0.7 copy.12
  (1 shorter events, 0.0 us)
Async XLA Ops:
  110.9 4.5 %copy-start = (f32[98,512]{1,0:T(8,128)S(1)}, f32[98,512]{1,0:T(8,128)}, u32[]{:S(2)}) copy-start(f32[98,512]{1,0:T(8,128)} %get-tuple-element.14) | copy-start | bytes 602116

commit v2 on v1

--- a/solution.py
+++ b/solution.py
@@ -28,7 +28,7 @@
 W_CHUNK = 1792
 N_W = F // W_CHUNK
 JA = 1024
-JB = 1024
+JB = 2048
 JC = 512
 
 ORDERS = ((0, 1, 2), (1, 2, 0), (2, 0, 1), (0, 2, 1))
@@ -52,10 +52,11 @@
 
 
 def kernel(
-    feat, w_hbm, centers_hbm, labels,
+    feat, w_hbm, centers_hbm, labels_in,
     loss_out, fc_out, gc_hbm,
+    labels,
     E, cen, clow, ct, tt, emb, gemb, gt, G, rb0, gs, rb1, gs2, rb2, gs3, rb3, cols,
-    own_emb, ar_send, ar_recv, rows,
+    cols_t, fc_send, fc_recv, own_emb, ar_send, ar_recv, rows,
     w_sem, c_sem, out_sem, ag_send, ag_recv, d_send, d_recv, rs_send, rs_recv,
     s_send, s_recv, a_send, a_recv,
 ):
@@ -63,7 +64,7 @@
     core = me[3]
     idx = ((me[0] * 4 + me[1]) * 4 + me[2]) * 2 + core
     offset = idx * CLASSES
-    place = core * (N // 2) + idx // 2
+    chip = idx // 2
 
     def peer(axis, k):
         size = 2 if axis == 3 else 4
@@ -88,6 +89,17 @@
         for k in (1, 2, 3):
             pl.semaphore_signal(barrier, inc=1, device_id=peer(axis, k), device_id_type=MESH)
     pl.semaphore_signal(barrier, inc=1, device_id=peer(3, 1), device_id_type=MESH)
+
+    lane = lax.broadcasted_iota(jnp.int32, (16, 128), 1)
+    for c in range(2):
+        low = labels_in[...]
+        for m in range(4):
+            moved = pltpu.roll(labels_in[...], (-16 * m - 16 * c) % 128, 1)
+            low = jnp.where(lane // 16 == m, moved, low)
+        high = pltpu.roll(low, 64, 1)
+        for g in range(8):
+            line = jnp.where(lane[0:1] < 64, low[2 * g : 2 * g + 1], high[2 * g + 1 : 2 * g + 2])
+            labels[2 * c + g // 4 : 2 * c + g // 4 + 1, (g % 4) * 128 : (g % 4 + 1) * 128] = line
 
     acc = jnp.zeros((OWN, D), f32)
     for i in range(N_W):
@@ -118,15 +130,18 @@
             device_id=peer(order[s], k), device_id_type=MESH,
         )
 
-    def ag_start(buf, inst, s):
+    def ag_start(buf, inst, p, s):
         for k in (1, 2, 3):
-            for p in range(4):
-                ag_copy(buf, inst, p, s, k).start()
-
-    def ag_wait(buf, inst, s):
-        for k in (1, 2, 3):
-            for p in range(4):
+            ag_copy(buf, inst, p, s, k).start()
+
+    def ag_next(buf, inst, s):
+        for p in range(4):
+            for k in (1, 2, 3):
                 ag_copy(buf, inst, p, s, k).wait_recv()
+            if s < 2:
+                ag_start(buf, inst, p, s + 1)
+            elif inst == 0:
+                pair_copy(buf, inst, p).start()
 
     def ag_drain(buf, inst):
         for s in range(3):
@@ -142,10 +157,6 @@
             device_id=peer(3, 1), device_id_type=MESH,
         )
 
-    def pair_start(buf, inst):
-        for p in range(4):
-            pair_copy(buf, inst, p).start()
-
     def pair_wait(buf, inst):
         for p in range(4):
             pair_copy(buf, inst, p).wait()
@@ -156,7 +167,8 @@
 
     put_own(emb, own_low)
     pl.semaphore_wait(barrier, 10)
-    ag_start(emb, 0, 0)
+    for p in range(4):
+        ag_start(emb, 0, p, 0)
 
     c_copy.wait()
 
@@ -169,63 +181,79 @@
         clow[r, :] = low
         ct[:, r] = last_dims(eye(D), low).astype(bf16)
 
-    ag_wait(emb, 0, 0)
-    ag_start(emb, 0, 1)
-
-    def target_rows(bt):
+    ag_next(emb, 0, 0)
+
+    @pl.loop(0, 4)
+    def _(bt):
         lab = labels[pl.ds(bt, 1), :] - offset
-        gt[bt] = jnp.zeros((D, BT), f32)
-
-        @pl.loop(0, CLASSES // JB)
-        def _(j):
-            j0 = pl.multiple_of(j * JB, JB)
+        total = jnp.zeros((D, BT), f32)
+        for j0 in range(0, CLASSES, JB):
             hot = (lab - j0) == lax.broadcasted_iota(jnp.int32, (JB, BT), 0)
             hot = jnp.where(hot, 1.0, 0.0).astype(bf16)
-            gt[bt] += plain_dot(ct[:, pl.ds(j0, JB)], hot)
-
-        tt[bt] = gt[bt].astype(bf16)
-
-    @pl.loop(0, 4)
-    def _(bt):
-        target_rows(bt)
+            total = total + plain_dot(ct[:, j0 : j0 + JB], hot)
+        tt[bt] = total.astype(bf16)
 
         @pl.when(bt == 0)
         def _():
-            ag_wait(emb, 0, 1)
-            ag_start(emb, 0, 2)
-
-    ag_wait(emb, 0, 2)
-    pair_start(emb, 0)
-    pair_wait(emb, 0)
-
-    def tile_of(dev):
-        return jnp.minimum((dev * F_DEV) // 128, F // 128 - 2)
-
-    def feature_copy(dev):
-        coords = (dev // 32, lax.rem(dev // 8, 4), lax.rem(dev // 2, 4), lax.rem(dev, 2))
+            ag_next(emb, 0, 1)
+
+    ag_next(emb, 0, 2)
+
+    def tile_of(c):
+        return jnp.minimum((c * 2 * F_DEV) // 128, F // 128 - 3)
+
+    def feature_copy(k):
+        to = lax.bitwise_and(chip + k, N // 2 - 1)
+        coords = (
+            lax.shift_right_logical(to, 4), lax.bitwise_and(lax.shift_right_logical(to, 2), 3), lax.bitwise_and(to, 3), core
+        )
         return pltpu.make_async_remote_copy(
-            src_ref=feat.at[:, pl.ds(pl.multiple_of(tile_of(dev) * 128, 128), 256)],
-            dst_ref=cols.at[place],
+            src_ref=feat.at[:, pl.ds(pl.multiple_of(tile_of(to) * 128, 128), 384)],
+            dst_ref=cols.at[chip],
             send_sem=a_send, recv_sem=a_recv, device_id=coords, device_id_type=MESH,
         )
 
-    cols[place] = feat[:, pl.ds(pl.multiple_of(tile_of(idx) * 128, 128), 256)]
-
-    @pl.loop(1, N)
-    def _(k):
-        feature_copy(lax.rem(idx + k, N)).start()
+    cols[chip] = feat[:, pl.ds(pl.multiple_of(tile_of(chip) * 128, 128), 384)]
 
     rows[...] = jnp.zeros_like(rows)
-
-    @pl.loop(0, 4 * (CLASSES // JA))
-    def _(i):
-        bt, j0 = i // (CLASSES // JA), pl.multiple_of(lax.rem(i, CLASSES // JA) * JA, JA)
-        cosines = last_dims(clow[pl.ds(j0, JA), :], block(emb, bt))
+    n_a = CLASSES // JA
+    tiles = 4 * n_a
+
+    def tile_at(t):
+        bt = lax.rem(t // n_a + 2 * core, 4)
+        return bt, pl.multiple_of(lax.rem(t, n_a) * JA, JA)
+
+    def cosine_tile(t, slot):
+        bt, j0 = tile_at(t)
+        gt[2 * slot : 2 * slot + 2] = last_dims(clow[pl.ds(j0, JA), :], block(emb, bt)).reshape(2, BT, BT)
+
+    def exp_tile(t, slot):
+        bt, j0 = tile_at(t)
+        cosines = gt[2 * slot : 2 * slot + 2].reshape(JA, BT)
         lab = labels[pl.ds(bt, 1), :] - offset - j0
         hot = lab == lax.broadcasted_iota(jnp.int32, (JA, BT), 0)
         e = jnp.where(hot, 0.0, jnp.exp2(cosines * exp2_scale))
         rows[bt] += jnp.sum(e.reshape(JA // 8, 8, BT), axis=0)
         E[bt, pl.ds(j0, JA), :] = e.astype(bf16)
+
+    cosine_tile(0, 0)
+
+    @pl.loop(0, tiles // 2 - 1)
+    def _(m):
+        @pl.when(m == tiles // 4 - 1)
+        def _():
+            pair_wait(emb, 0)
+
+        for u in range(9):
+            feature_copy(m * 9 + u + 1).start()
+        cosine_tile(2 * m + 1, 1)
+        exp_tile(2 * m, 0)
+        cosine_tile(2 * m + 2, 0)
+        exp_tile(2 * m + 1, 1)
+
+    cosine_tile(tiles - 1, 1)
+    exp_tile(tiles - 2, 0)
+    exp_tile(tiles - 1, 1)
 
     target = []
     for bt in range(4):
@@ -268,16 +296,13 @@
     ar_start(0)
 
     @pl.loop(0, 4)
-    def _(bt):
-        gt[bt] = jnp.zeros((D, BT), f32)
-
-        @pl.loop(0, CLASSES // JB)
-        def _(j):
-            j0 = pl.multiple_of(j * JB, JB)
-            gt[bt] += plain_dot(ct[:, pl.ds(j0, JB)], E[bt, pl.ds(j0, JB), :])
-
+    def _(i):
+        bt = lax.rem(i + 2 * core + 2, 4)
+        for h in range(CLASSES // JB):
+            part = plain_dot(ct[:, h * JB : (h + 1) * JB], E[bt, h * JB : (h + 1) * JB, :])
+            gt[bt] = part if h == 0 else gt[bt] + part
         for s in range(4):
-            @pl.when(bt == s)
+            @pl.when(i == s)
             def _():
                 ar_finish(s)
                 if s < 3:
@@ -327,17 +352,16 @@
             device_id=to, device_id_type=MESH,
         )
 
-    def rs_start(s):
+    def rs_start(s, p):
         for k in (1, 2, 3):
-            for p in range(4):
-                rs_copy(s, p, k).start()
+            rs_copy(s, p, k).start()
 
     def rs_step(stage):
         if stage == 0:
             for p in range(4):
                 rs0_copy(p).wait()
                 gs[p] = (G[p, core].astype(f32) + rb0[p].astype(f32)).astype(bf16)
-            rs_start(0)
+                rs_start(0, p)
             return None
         s = stage - 1
         out = []
@@ -359,12 +383,13 @@
                 total = total + bufs[p, k - 1].astype(f32)
             if s == 0:
                 gs2[p] = total.astype(bf16)
+                rs_start(1, p)
             elif s == 1:
                 gs3[p] = total.astype(bf16)
+                rs_start(2, p)
             else:
                 out.append(total)
         if s < 2:
-            rs_start(s + 1)
             return None
         for s in range(3):
             for p in range(4):
@@ -379,30 +404,32 @@
         direction = own * inv
         along = jnp.sum(grad_dir * direction, axis=1, keepdims=True)
         put_own(gemb, ((grad_dir - direction * along) * inv).astype(bf16))
-        ag_start(gemb, 1, 0)
-
-    def ag_step(s):
-        ag_wait(gemb, 1, s)
-        if s < 2:
-            ag_start(gemb, 1, s + 1)
-        else:
-            pair_start(gemb, 1)
+        for p in range(4):
+            ag_start(gemb, 1, p, 0)
 
     for p in range(4):
         rs0_copy(p).start()
 
     def out_copy(i):
         r = pl.ds(pl.multiple_of(i * JC, JC), JC)
-        return pltpu.make_async_copy(cen.at[r], gc_hbm.at[r], out_sem.at[i])
+        return pltpu.make_async_copy(clow.at[r], gc_hbm.at[r], out_sem.at[i])
 
     steps = {
         0: functools.partial(rs_step, 0),
         2: functools.partial(rs_step, 1),
         4: functools.partial(rs_step, 2),
         5: owner_step,
-        6: functools.partial(ag_step, 0),
-        7: functools.partial(ag_step, 1),
+        6: functools.partial(ag_next, gemb, 1, 0),
+        7: functools.partial(ag_next, gemb, 1, 1),
     }
+
+    def finish_centers(i, slot):
+        r = pl.ds(pl.multiple_of(i * JC, JC), JC)
+        gu = gt[slot]
+        cf = cen[r, :].astype(f32)
+        inv = lax.rsqrt(jnp.sum(cf * cf, axis=1, keepdims=True) + epsilon)
+        along = jnp.sum(gu * cf, axis=1, keepdims=True) * (inv * inv * inv)
+        clow[r, :] = (gu * inv - cf * along).astype(bf16)
 
     @pl.loop(0, CLASSES // JC)
     def _(i):
@@ -415,34 +442,46 @@
             scaled = E[bt, r, :].astype(f32) * rows[bt, 0:1, :]
             gc = jnp.where(hot, rows[bt, 1:2, :], scaled).astype(bf16)
             gu = gu + plain_dot(gc, block(emb, bt))
-        cf = cen[r, :].astype(f32)
-        inv = lax.rsqrt(jnp.sum(cf * cf, axis=1, keepdims=True) + epsilon)
-        cdir = cf * inv
-        along = jnp.sum(gu * cdir, axis=1, keepdims=True)
-        cen[r, :] = ((gu - cdir * along) * inv).astype(bf16)
-        out_copy(i).start()
+        gt[lax.rem(i, 2)] = gu
+        before = jnp.maximum(i - 1, 0)
+        finish_centers(before, lax.rem(i + 1, 2))
+
+        @pl.when(i > 0)
+        def _():
+            out_copy(before).start()
+
         for at, step in steps.items():
             @pl.when(i == at)
             def _():
                 step()
 
-    ag_step(2)
-
-    others = cols.at[pl.ds(0, N - 1)]
+    finish_centers(CLASSES // JC - 1, (CLASSES // JC - 1) % 2)
+    out_copy(CLASSES // JC - 1).start()
+
+    others = cols.at[pl.ds(0, N // 2 - 1)]
     pltpu.make_async_copy(others, others, a_send).wait()
     pltpu.make_async_copy(others, others, a_recv).wait()
 
-    start = idx * F_DEV - tile_of(idx) * 128
-    pick = lax.broadcasted_iota(jnp.int32, (104, 256), 1) == lax.broadcasted_iota(jnp.int32, (104, 256), 0) + start
-    pick = pick.astype(f32).astype(bf16)
-    mine = [
-        last_dims(pick, cols[bt * 32 : (bt + 1) * 32].reshape(BT, 256)).astype(bf16) for bt in range(4)
-    ]
-    pair_wait(gemb, 1)
-    fc = jnp.zeros((104, D), f32)
-    for bt in range(4):
-        fc = fc + plain_dot(mine[bt], block(gemb, bt))
-    fc_out[...] = fc[0:F_DEV]
+    start = chip * 2 * F_DEV - tile_of(chip) * 128
+    r = lax.broadcasted_iota(jnp.int32, (208, 384), 0)
+    want = start + jnp.where(r < 104, core * F_DEV + r, (1 - core) * F_DEV + r - 104)
+    pick = (lax.broadcasted_iota(jnp.int32, (208, 384), 1) == want).astype(f32).astype(bf16)
+    for h in range(2):
+        cols_t[h] = last_dims(pick, cols[h * 32 : (h + 1) * 32].reshape(BT, 384)).astype(bf16)
+
+    ag_next(gemb, 1, 2)
+    fc = jnp.zeros((208, D), f32)
+    for h in range(2):
+        rows_h = jnp.concatenate([gemb[p, core, 2 * h : 2 * h + 2].reshape(BT, 128) for p in range(4)], axis=1)
+        fc = fc + plain_dot(cols_t[h], rows_h)
+    fc_send[...] = fc[104:208]
+    fc_copy = pltpu.make_async_remote_copy(
+        src_ref=fc_send, dst_ref=fc_recv, send_sem=d_send.at[1, 0], recv_sem=d_recv.at[1, 0],
+        device_id=peer(3, 1), device_id_type=MESH,
+    )
+    fc_copy.start()
+    fc_copy.wait()
+    fc_out[...] = (fc[0:104] + fc_recv[...])[0:F_DEV]
 
     for i in range(CLASSES // JC):
         out_copy(i).wait()
@@ -450,8 +489,32 @@
     ag_drain(gemb, 1)
 
 
+def emit_kernel(loss_all, fc, gc_hbm, loss_out, fc_out, out_hbm, held, in_sem, out_sem):
+    step = CLASSES // 8
+
+    def read(i):
+        r = pl.ds(i * step, step)
+        return pltpu.make_async_copy(gc_hbm.at[r], held.at[r], in_sem.at[i])
+
+    def write(i):
+        r = pl.ds(i * step, step)
+        return pltpu.make_async_copy(held.at[r], out_hbm.at[r], out_sem.at[i])
+
+    for i in range(8):
+        read(i).start()
+    chip = (lax.axis_index("cls_0") * 4 + lax.axis_index("cls_1")) * 4 + lax.axis_index("cls_2")
+    position = lax.axis_index("cls_3") * 64 + chip
+    line = loss_all[pl.ds(position // 32, 1), :]
+    loss_out[...] = pltpu.roll(line, lax.rem(BT - lax.rem(position, 32) * OWN, BT), 1)[:, 0:OWN]
+    fc_out[...] = fc[...]
+    for i in range(8):
+        read(i).wait()
+        write(i).start()
+    for i in range(8):
+        write(i).wait()
+
+
 def on_device(features, fc_weight, centers, labels):
-    ordered = labels.reshape(64, 2, OWN).transpose(1, 0, 2).reshape(4, BT)
     vmem = pl.BlockSpec(memory_space=pltpu.VMEM)
     anywhere = pl.BlockSpec(memory_space=pl.ANY)
     dma = pltpu.SemaphoreType.DMA
@@ -465,6 +528,7 @@
         in_specs=[vmem, anywhere, anywhere, vmem],
         out_specs=(vmem, vmem, anywhere),
         scratch_shapes=[
+            pltpu.VMEM((4, BT), jnp.int32),
             pltpu.VMEM((4, CLASSES, BT), bf16),
             pltpu.VMEM((CLASSES, D), bf16),
             pltpu.VMEM((CLASSES, D), bf16),
@@ -481,7 +545,10 @@
             pltpu.VMEM((4, 3, 4, OWN, 128), bf16),
             pltpu.VMEM((4, 4, OWN, 128), bf16),
             pltpu.VMEM((4, 3, OWN, 128), bf16),
-            pltpu.VMEM((N, OWN, 256), bf16),
+            pltpu.VMEM((N // 2, OWN, 384), bf16),
+            pltpu.VMEM((2, 208, BT), bf16),
+            pltpu.VMEM((104, D), f32),
+            pltpu.VMEM((104, D), f32),
             pltpu.VMEM((OWN, D), f32),
             pltpu.VMEM((5, 8, BT), f32),
             pltpu.VMEM((4, 3, 8, BT), f32),
@@ -503,10 +570,19 @@
         compiler_params=pltpu.CompilerParams(
             collective_id=0, has_side_effects=True, vmem_limit_bytes=66_000_000
         ),
-    )(features, fc_weight, centers, ordered)
-    position = (lax.axis_index("cls_3") * 64 + lax.axis_index(CLS[:3])) * OWN
-    loss = lax.dynamic_slice_in_dim(loss_all.reshape(-1), position, OWN)
-    return (loss, grad_centers, grad_fc)
+    )(features, fc_weight, centers, labels.reshape(16, 128))
+    loss, grad_fc, grad_centers = pl.pallas_call(
+        emit_kernel,
+        out_shape=(
+            jax.ShapeDtypeStruct((1, OWN), f32),
+            jax.ShapeDtypeStruct((F_DEV, D), f32),
+            jax.ShapeDtypeStruct((CLASSES, D), bf16),
+        ),
+        in_specs=[vmem, vmem, anywhere],
+        out_specs=(vmem, vmem, anywhere),
+        scratch_shapes=[pltpu.VMEM((CLASSES, D), bf16), dma((8,)), dma((8,))],
+    )(loss_all, grad_fc, grad_centers)
+    return (loss.reshape(-1), grad_centers, grad_fc)
 
 
 def solution(mesh):

time: 116 us -> 101 us (0.87)
  local copies, waits for them, and re-layouts: 8.01 us -> 0 us
  Pallas kernels: 107 us -> 101 us
    pallas_call x1, Pallas kernels: 107 us -> 95.3 us  [on_device(): pl.pallas_call(kernel, out_shape=(jax.ShapeDtypeStruct((4, BT), f32), jax...]
    unnamed x5 -> x0, local copies, waits for them, and re-layouts: 5.9 us -> none
    pallas_call x0 -> x1, Pallas kernels: none -> 5.23 us  [on_device(): pl.pallas_call(emit_kernel, out_shape=(jax.ShapeDtypeStruct((1, OWN), f32...]
    reshape x2 -> x0, local copies, waits for them, and re-layouts: 1.52 us -> none  [on_device(): ordered = labels.reshape(64, 2, OWN).transpose(1, 0, 2).reshape(4, BT)]
where the time goes in v2:
time: 101 us
  Pallas kernels  101 us (100%)
    pallas_call x1, Pallas kernels, on_device(): pl.pallas_call(kernel, out_shape=(jax.ShapeDtypeStruct((4, BT), f32), jax...  95.3 us
    pallas_call x1, Pallas kernels, on_device(): pl.pallas_call(emit_kernel, out_shape=(jax.ShapeDtypeStruct((1, OWN), f32...  5.23 us

profile of v2, /device:TPU:1, one launch (start us, length us, event | category | flops | bytes accessed | tf_op | source)
XLA Modules:
  0.0 101.2 jit_solution(15456785350222001040)
XLA Ops:
  0.6 95.3 %shard_map.67 = (f32[4,512]{1,0:T(4,128)}, f32[98,512]{1,0:T(8,128)}, bf16[4096,512]{1,0:T(8,128)(2,1)}) custom-call(bf16[16,12544]{1,0:T(8,128)(2,1)} %feat.1, bf16[12544,512]{1,0:T(8,128)(2,1)} %w_hbm.1, bf16[4096,512]{1,0:T(8,128)(2,1)} %centers_hbm.1, s32[16,128]{1,0:T(8,128)} %bitcast.2), custom_call_target="tpu_custom_call" | custom-call | tf_op jit(solution)/shard_map/pallas_call | solution.py:521
  96.0 5.2 %shard_map.68 = (f32[1,16]{1,0:T(1,128)}, f32[98,512]{1,0:T(8,128)}, bf16[4096,512]{1,0:T(8,128)(2,1)}) custom-call(f32[4,512]{1,0:T(4,128)} %get-tuple-element.9.loss_all, f32[98,512]{1,0:T(8,128)} %get-tuple-element.10.fc, bf16[4096,512]{1,0:T(8,128)(2,1)} %get-tuple-element.11.gc_hbm), custom_call_target="tpu_custom_call" | custom-call | tf_op jit(solution)/shard_map/pallas_call | solution.py:574

commit v3 on v2

--- a/solution.py
+++ b/solution.py
@@ -31,7 +31,7 @@
 JB = 2048
 JC = 512
 
-ORDERS = ((0, 1, 2), (1, 2, 0), (2, 0, 1), (0, 2, 1))
+ORDERS = ((0, 1, 2), (1, 2, 0), (2, 0, 1), (0, 2, 1), (0, 1, 2))
 
 f32 = jnp.float32
 bf16 = jnp.bfloat16
@@ -43,6 +43,12 @@
 
 def plain_dot(a, b):
     return lax.dot_general(a, b, (((1,), (0,)), ((), ())), preferred_element_type=f32)
+
+
+def transposed(x):
+    width = x.shape[1]
+    one = eye(256)
+    return jnp.concatenate([last_dims(one, x[:, c : c + 256]) for c in range(0, width, 256)], axis=0).astype(bf16)
 
 
 def eye(n):
@@ -55,7 +61,7 @@
     feat, w_hbm, centers_hbm, labels_in,
     loss_out, fc_out, gc_hbm,
     labels,
-    E, cen, clow, ct, tt, emb, gemb, gt, G, rb0, gs, rb1, gs2, rb2, gs3, rb3, cols,
+    E, cen, clow, ct, tt, ttr, emb, gemb, gt, gsend, grecv, gs, rb1, gs2, rb2, gs3, rb3, rs_out, cols,
     cols_t, fc_send, fc_recv, own_emb, ar_send, ar_recv, rows,
     w_sem, c_sem, out_sem, ag_send, ag_recv, d_send, d_recv, rs_send, rs_recv,
     s_send, s_recv, a_send, a_recv,
@@ -121,8 +127,16 @@
         where = tuple(slice(None) if a in gathered else at[a] for a in range(3))
         return buf.at[(p, core) + where]
 
-    def ag_copy(buf, inst, p, s, k):
-        order = ORDERS[p]
+    def by_order(p, act):
+        if p < 3:
+            act(ORDERS[p])
+            return
+        for c in range(2):
+            @pl.when(core == c)
+            def _():
+                act(ORDERS[3 + c])
+
+    def ag_copy(buf, inst, p, s, k, order):
         v = view(buf, p, order[:s])
         return pltpu.make_async_remote_copy(
             src_ref=v, dst_ref=v,
@@ -131,13 +145,16 @@
         )
 
     def ag_start(buf, inst, p, s):
-        for k in (1, 2, 3):
-            ag_copy(buf, inst, p, s, k).start()
+        def act(order):
+            for k in (1, 2, 3):
+                ag_copy(buf, inst, p, s, k, order).start()
+
+        by_order(p, act)
 
     def ag_next(buf, inst, s):
         for p in range(4):
             for k in (1, 2, 3):
-                ag_copy(buf, inst, p, s, k).wait_recv()
+                ag_copy(buf, inst, p, s, k, ORDERS[p]).wait_recv()
             if s < 2:
                 ag_start(buf, inst, p, s + 1)
             elif inst == 0:
@@ -147,7 +164,7 @@
         for s in range(3):
             for k in (1, 2, 3):
                 for p in range(4):
-                    ag_copy(buf, inst, p, s, k).wait_send()
+                    ag_copy(buf, inst, p, s, k, ORDERS[p]).wait_send()
 
     def pair_copy(buf, inst, p):
         v = buf.at[p, core]
@@ -179,9 +196,11 @@
         inv = lax.rsqrt(jnp.sum(cf * cf, axis=1, keepdims=True) + epsilon)
         low = (cf * inv).astype(bf16)
         clow[r, :] = low
-        ct[:, r] = last_dims(eye(D), low).astype(bf16)
-
-    ag_next(emb, 0, 0)
+        ct[:, r] = transposed(low)
+
+        @pl.when(i == 4)
+        def _():
+            ag_next(emb, 0, 0)
 
     @pl.loop(0, 4)
     def _(bt):
@@ -199,6 +218,13 @@
 
     ag_next(emb, 0, 2)
 
+    def tt_copy():
+        return pltpu.make_async_remote_copy(
+            src_ref=tt.at[pl.ds(2 * (1 - core), 2)], dst_ref=ttr,
+            send_sem=d_send.at[1, 1], recv_sem=d_recv.at[1, 1], device_id=peer(3, 1), device_id_type=MESH,
+        )
+
+    tt_copy().start()
     def tile_of(c):
         return jnp.minimum((c * 2 * F_DEV) // 128, F // 128 - 3)
 
@@ -255,85 +281,113 @@
     exp_tile(tiles - 2, 0)
     exp_tile(tiles - 1, 1)
 
-    target = []
-    for bt in range(4):
-        lab = labels[bt : bt + 1, :] - offset
-        here = jnp.logical_and(lab >= 0, lab < CLASSES)
-        emb_t = last_dims(eye(D), block(emb, bt))
-        tc = jnp.sum(emb_t * tt[bt].astype(f32), axis=0, keepdims=True)
+    def margin(tc):
         ts = jnp.sqrt(1.0 - tc * tc)
         margined = logit_scale * (tc * cos_margin - ts * sin_margin)
-        slope = cos_margin + sin_margin * tc / ts
-        e_t = jnp.where(here, jnp.exp(margined), 0.0)
-        slope = jnp.where(here, slope, 0.0)
-        target.append((e_t, slope))
-        ar_send[0, bt : bt + 1, :] = jnp.sum(rows[bt], axis=0, keepdims=True) + e_t
-        ar_send[0, 4 + bt : 5 + bt, :] = jnp.where(here, margined, 0.0)
-
-    AR_AXES = (3, 2, 1, 0)
-
-    def ar_copy(s, k):
+        return margined, cos_margin + sin_margin * tc / ts
+
+    def on_chip(bt):
+        lab = labels[pl.ds(bt, 1), :] - chip * (2 * CLASSES)
+        return jnp.logical_and(lab >= 0, lab < 2 * CLASSES)
+
+    ar_send[0, 4:8, :] = jnp.zeros((4, BT), f32)
+    for bt in range(4):
+        ar_send[0, bt : bt + 1, :] = jnp.sum(rows[bt], axis=0, keepdims=True)
+    tt_copy().wait()
+    for h in range(2):
+        bt = 2 * core + h
+        rows_t = tt[bt].astype(f32) + ttr[h].astype(f32)
+        ttr[h] = rows_t.astype(bf16)
+        own_rows = jnp.concatenate([emb[p, core, 2 * h : 2 * h + 2].reshape(BT, 128) for p in range(4)], axis=1)
+        tc = jnp.sum(transposed(own_rows).astype(f32) * rows_t, axis=0, keepdims=True)
+        margined, _ = margin(tc)
+        ar_send[0, pl.ds(bt, 1), :] += jnp.where(on_chip(bt), jnp.exp(margined), 0.0)
+        ar_send[0, pl.ds(4 + bt, 1), :] = tc
+
+    AR_PEERS = (
+        tuple((z, c) for z in range(4) for c in range(2) if z + c > 0),
+        tuple((1, k) for k in (1, 2, 3)),
+        tuple((0, k) for k in (1, 2, 3)),
+    )
+
+    def ar_copy(s, n):
+        if s == 0:
+            dz, dc = AR_PEERS[0][n]
+            to = (me[0], me[1], lax.rem(me[2] + dz, 4), lax.rem(core + dc, 2))
+        else:
+            to = peer(*AR_PEERS[s][n])
         return pltpu.make_async_remote_copy(
-            src_ref=ar_send.at[s], dst_ref=ar_recv.at[s, k - 1],
-            send_sem=s_send.at[s, k - 1], recv_sem=s_recv.at[s, k - 1],
-            device_id=peer(AR_AXES[s], k), device_id_type=MESH,
-        )
-
-    def ar_peers(s):
-        return (1,) if s == 0 else (1, 2, 3)
+            src_ref=ar_send.at[s], dst_ref=ar_recv.at[s, n],
+            send_sem=s_send.at[s, n], recv_sem=s_recv.at[s, n],
+            device_id=to, device_id_type=MESH,
+        )
 
     def ar_start(s):
-        for k in ar_peers(s):
-            ar_copy(s, k).start()
+        for n in range(len(AR_PEERS[s])):
+            ar_copy(s, n).start()
 
     def ar_finish(s):
         total = ar_send[s]
-        for k in ar_peers(s):
-            ar_copy(s, k).wait_recv()
-            total = total + ar_recv[s, k - 1]
+        for n in range(len(AR_PEERS[s])):
+            ar_copy(s, n).wait_recv()
+            total = total + ar_recv[s, n]
         ar_send[s + 1] = total
+        if s < 2:
+            ar_start(s + 1)
 
     ar_start(0)
+
+    def g_copy(h):
+        return pltpu.make_async_remote_copy(
+            src_ref=gsend.at[h], dst_ref=grecv.at[h],
+            send_sem=d_send.at[2, h], recv_sem=d_recv.at[2, h], device_id=peer(3, 1), device_id_type=MESH,
+        )
+
+    half = CLASSES // 2
 
     @pl.loop(0, 4)
     def _(i):
         bt = lax.rem(i + 2 * core + 2, 4)
-        for h in range(CLASSES // JB):
-            part = plain_dot(ct[:, h * JB : (h + 1) * JB], E[bt, h * JB : (h + 1) * JB, :])
-            gt[bt] = part if h == 0 else gt[bt] + part
-        for s in range(4):
-            @pl.when(i == s)
-            def _():
-                ar_finish(s)
-                if s < 3:
-                    ar_start(s + 1)
-
-    for s in range(4):
-        for k in ar_peers(s):
-            ar_copy(s, k).wait_send()
+        gt[i] = plain_dot(ct[:, 0:half], E[bt, 0:half, :])
+
+        @pl.when(i == 1)
+        def _():
+            ar_finish(0)
+
+        gt[i] += plain_dot(ct[:, half:], E[bt, half:, :])
+
+        @pl.when(i == 2)
+        def _():
+            ar_finish(1)
+
+        @pl.when(i < 2)
+        def _():
+            gsend[i] = gt[i].astype(bf16)
+            g_copy(i).start()
+
+    ar_finish(2)
+    for s in range(3):
+        for n in range(len(AR_PEERS[s])):
+            ar_copy(s, n).wait_send()
 
     for bt in range(4):
-        total = ar_send[4, bt : bt + 1, :]
-        loss_out[bt : bt + 1, :] = jnp.log(total) - ar_send[4, 4 + bt : 5 + bt, :]
-        e_t, slope = target[bt]
+        total = ar_send[3, bt : bt + 1, :]
+        margined, slope = margin(ar_send[3, 4 + bt : 5 + bt, :])
+        loss_out[bt : bt + 1, :] = jnp.log(total) - margined
         scale = logit_scale / total
-        v = (e_t - total) * slope * scale
         rows[bt, 0:1, :] = scale
-        rows[bt, 1:2, :] = v
-        g = (gt[bt] * scale + v * tt[bt].astype(f32)).astype(bf16)
-        back = last_dims(eye(BT), g).astype(bf16)
+        rows[bt, 1:2, :] = (jnp.exp(margined) - total) * slope * scale
+
+    for h in range(2):
+        bt = 2 * core + h
+        g_copy(h).wait()
+        v = jnp.where(on_chip(bt), rows[bt, 1:2, :], 0.0)
+        g = (gt[2 + h] + grecv[h].astype(f32)) * rows[bt, 0:1, :] + v * ttr[h].astype(f32)
+        back = transposed(g.astype(bf16))
         for p in range(4):
-            G[p, bt // 2, (bt % 2) * 2 : (bt % 2) * 2 + 2] = back[:, p * 128 : (p + 1) * 128].reshape(2, 4, 4, OWN, 128)
-
-    def rs0_copy(p):
-        return pltpu.make_async_remote_copy(
-            src_ref=G.at[p, 1 - core], dst_ref=rb0.at[p],
-            send_sem=d_send.at[2, p], recv_sem=d_recv.at[2, p],
-            device_id=peer(3, 1), device_id_type=MESH,
-        )
-
-    def rs_copy(s, p, k):
-        order = ORDERS[p]
+            gs[p, 2 * h : 2 * h + 2] = back[:, p * 128 : (p + 1) * 128].reshape(2, 4, 4, OWN, 128)
+
+    def rs_copy(s, p, k, order):
         axis = order[2 - s]
         to = peer(axis, k)
         if s == 0:
@@ -353,52 +407,44 @@
         )
 
     def rs_start(s, p):
-        for k in (1, 2, 3):
-            rs_copy(s, p, k).start()
-
-    def rs_step(stage):
-        if stage == 0:
-            for p in range(4):
-                rs0_copy(p).wait()
-                gs[p] = (G[p, core].astype(f32) + rb0[p].astype(f32)).astype(bf16)
-                rs_start(0, p)
-            return None
-        s = stage - 1
-        out = []
+        def act(order):
+            for k in (1, 2, 3):
+                rs_copy(s, p, k, order).start()
+
+        by_order(p, act)
+
+    def rs_step(s):
+        bufs = (rb1, rb2, rb3)[s]
         for p in range(4):
-            order = ORDERS[p]
-            axis = order[2 - s]
-            if s == 0:
-                total = gs[(p,) + tuple(me[a] if a == axis else slice(None) for a in range(3))]
-                bufs = rb1
-            elif s == 1:
-                total = gs2[(p,) + tuple(me[a] if a == axis else slice(None) for a in sorted(order[:2]))]
-                bufs = rb2
-            else:
-                total = gs3[p, me[axis]]
-                bufs = rb3
-            total = total.astype(f32)
             for k in (1, 2, 3):
-                rs_copy(s, p, k).wait_recv()
-                total = total + bufs[p, k - 1].astype(f32)
-            if s == 0:
-                gs2[p] = total.astype(bf16)
-                rs_start(1, p)
-            elif s == 1:
-                gs3[p] = total.astype(bf16)
-                rs_start(2, p)
-            else:
-                out.append(total)
-        if s < 2:
-            return None
-        for s in range(3):
-            for p in range(4):
+                rs_copy(s, p, k, ORDERS[p]).wait_recv()
+
+            def act(order):
+                axis = order[2 - s]
+                if s == 0:
+                    total = gs[(p,) + tuple(me[a] if a == axis else slice(None) for a in range(3))]
+                elif s == 1:
+                    total = gs2[(p,) + tuple(me[a] if a == axis else slice(None) for a in sorted(order[:2]))]
+                else:
+                    total = gs3[p, me[axis]]
+                total = total.astype(f32)
                 for k in (1, 2, 3):
-                    rs_copy(s, p, k).wait_send()
-        return jnp.concatenate(out, axis=1)
+                    total = total + bufs[p, k - 1].astype(f32)
+                if s == 0:
+                    gs2[p] = total.astype(bf16)
+                elif s == 1:
+                    gs3[p] = total.astype(bf16)
+                else:
+                    rs_out[:, p * 128 : (p + 1) * 128] = total
+                if s < 2:
+                    for k in (1, 2, 3):
+                        rs_copy(s + 1, p, k, order).start()
+
+            by_order(p, act)
 
     def owner_step():
-        grad_dir = rs_step(3)
+        rs_step(2)
+        grad_dir = rs_out[...]
         own = own_emb[...]
         inv = lax.rsqrt(jnp.sum(own * own, axis=1, keepdims=True) + epsilon)
         direction = own * inv
@@ -408,19 +454,17 @@
             ag_start(gemb, 1, p, 0)
 
     for p in range(4):
-        rs0_copy(p).start()
+        rs_start(0, p)
 
     def out_copy(i):
         r = pl.ds(pl.multiple_of(i * JC, JC), JC)
         return pltpu.make_async_copy(clow.at[r], gc_hbm.at[r], out_sem.at[i])
 
     steps = {
-        0: functools.partial(rs_step, 0),
-        2: functools.partial(rs_step, 1),
-        4: functools.partial(rs_step, 2),
-        5: owner_step,
-        6: functools.partial(ag_next, gemb, 1, 0),
-        7: functools.partial(ag_next, gemb, 1, 1),
+        3: functools.partial(rs_step, 0),
+        5: functools.partial(rs_step, 1),
+        6: owner_step,
+        7: functools.partial(ag_next, gemb, 1, 0),
     }
 
     def finish_centers(i, slot):
@@ -458,6 +502,8 @@
     finish_centers(CLASSES // JC - 1, (CLASSES // JC - 1) % 2)
     out_copy(CLASSES // JC - 1).start()
 
+    ag_next(gemb, 1, 1)
+
     others = cols.at[pl.ds(0, N // 2 - 1)]
     pltpu.make_async_copy(others, others, a_send).wait()
     pltpu.make_async_copy(others, others, a_recv).wait()
@@ -487,6 +533,10 @@
         out_copy(i).wait()
     ag_drain(emb, 0)
     ag_drain(gemb, 1)
+    for s in range(3):
+        for p in range(4):
+            for k in (1, 2, 3):
+                rs_copy(s, p, k, ORDERS[p]).wait_send()
 
 
 def emit_kernel(loss_all, fc, gc_hbm, loss_out, fc_out, out_hbm, held, in_sem, out_sem):
@@ -534,24 +584,26 @@
             pltpu.VMEM((CLASSES, D), bf16),
             pltpu.VMEM((D, CLASSES), bf16),
             pltpu.VMEM((4, D, BT), bf16),
+            pltpu.VMEM((2, D, BT), bf16),
             pltpu.VMEM((4, 2, 4, 4, 4, OWN, 128), bf16),
             pltpu.VMEM((4, 2, 4, 4, 4, OWN, 128), bf16),
             pltpu.VMEM((4, D, BT), f32),
-            pltpu.VMEM((4, 2, 4, 4, 4, OWN, 128), bf16),
-            pltpu.VMEM((4, 4, 4, 4, OWN, 128), bf16),
+            pltpu.VMEM((2, D, BT), bf16),
+            pltpu.VMEM((2, D, BT), bf16),
             pltpu.VMEM((4, 4, 4, 4, OWN, 128), bf16),
             pltpu.VMEM((4, 3, 4, 4, OWN, 128), bf16),
             pltpu.VMEM((4, 4, 4, OWN, 128), bf16),
             pltpu.VMEM((4, 3, 4, OWN, 128), bf16),
             pltpu.VMEM((4, 4, OWN, 128), bf16),
             pltpu.VMEM((4, 3, OWN, 128), bf16),
+            pltpu.VMEM((OWN, D), f32),
             pltpu.VMEM((N // 2, OWN, 384), bf16),
             pltpu.VMEM((2, 208, BT), bf16),
             pltpu.VMEM((104, D), f32),
             pltpu.VMEM((104, D), f32),
             pltpu.VMEM((OWN, D), f32),
-            pltpu.VMEM((5, 8, BT), f32),
-            pltpu.VMEM((4, 3, 8, BT), f32),
+            pltpu.VMEM((4, 8, BT), f32),
+            pltpu.VMEM((3, 7, 8, BT), f32),
             pltpu.VMEM((4, 8, BT), f32),
             dma((N_W,)),
             dma,
@@ -562,8 +614,8 @@
             dma((3, 4)),
             dma((3, 4, 3)),
             dma((3, 4, 3)),
-            dma((4, 3)),
-            dma((4, 3)),
+            dma((3, 7)),
+            dma((3, 7)),
             dma,
             dma,
         ],

time: 101 us -> 93 us (0.921)
  Pallas kernels: 101 us -> 92.2 us
    pallas_call x1, Pallas kernels: 95.3 us -> 86.9 us  [on_device(): pl.pallas_call(kernel, out_shape=(jax.ShapeDtypeStruct((4, BT), f32), jax...]
where the time goes in v3:
time: 93 us; the launch traced here: 92.8 us
  Pallas kernels  92.2 us (99%)
    pallas_call x1, Pallas kernels, on_device(): pl.pallas_call(kernel, out_shape=(jax.ShapeDtypeStruct((4, BT), f32), jax...  86.9 us
    pallas_call x1, Pallas kernels, on_device(): pl.pallas_call(emit_kernel, out_shape=(jax.ShapeDtypeStruct((1, OWN), f32...  5.23 us

profile of v3, /device:TPU:1, one launch (start us, length us, event | category | flops | bytes accessed | tf_op | source)
XLA Modules:
  0.0 92.8 jit_solution(13092910956766493390)
XLA Ops:
  0.6 86.9 %shard_map.67 = (f32[4,512]{1,0:T(4,128)}, f32[98,512]{1,0:T(8,128)}, bf16[4096,512]{1,0:T(8,128)(2,1)}) custom-call(bf16[16,12544]{1,0:T(8,128)(2,1)} %feat.1, bf16[12544,512]{1,0:T(8,128)(2,1)} %w_hbm.1, bf16[4096,512]{1,0:T(8,128)(2,1)} %centers_hbm.1, s32[16,128]{1,0:T(8,128)} %bitcast.2), custom_call_target="tpu_custom_call" | custom-call | tf_op jit(solution)/shard_map/pallas_call | solution.py:571
  87.6 5.2 %shard_map.68 = (f32[1,16]{1,0:T(1,128)}, f32[98,512]{1,0:T(8,128)}, bf16[4096,512]{1,0:T(8,128)(2,1)}) custom-call(f32[4,512]{1,0:T(4,128)} %get-tuple-element.9.loss_all, f32[98,512]{1,0:T(8,128)} %get-tuple-element.10.fc, bf16[4096,512]{1,0:T(8,128)(2,1)} %get-tuple-element.11.gc_hbm), custom_call_target="tpu_custom_call" | custom-call | tf_op jit(solution)/shard_map/pallas_call | solution.py:626

commit v4 on v3

--- a/solution.py
+++ b/solution.py
@@ -58,12 +58,12 @@
 
 
 def kernel(
-    feat, w_hbm, centers_hbm, labels_in,
-    loss_out, fc_out, gc_hbm,
-    labels,
-    E, cen, clow, ct, tt, ttr, emb, gemb, gt, gsend, grecv, gs, rb1, gs2, rb2, gs3, rb3, rs_out, cols,
+    feat_hbm, w_hbm, centers_hbm, labels_hbm,
+    loss_out, fc_out, gc_out,
+    feat, labels_in, labels, losses,
+    E, cen, clow, ct, tt, ttr, emb, emb_t, gemb, gt, gsend, grecv, gs, rb1, gs2, rb2, gs3, rb3, rs_out, cols,
     cols_t, fc_send, fc_recv, own_emb, ar_send, ar_recv, rows,
-    w_sem, c_sem, out_sem, ag_send, ag_recv, d_send, d_recv, rs_send, rs_recv,
+    w_sem, c_sem, ag_send, ag_recv, d_send, d_recv, rs_send, rs_recv,
     s_send, s_recv, a_send, a_recv,
 ):
     me = tuple(lax.axis_index(name) for name in CLS)
@@ -85,17 +85,22 @@
             w_sem.at[i],
         )
 
-    c_copy = pltpu.make_async_copy(centers_hbm, cen, c_sem)
+    feat_fetch = pltpu.make_async_copy(feat_hbm, feat, c_sem.at[1])
+    labels_fetch = pltpu.make_async_copy(labels_hbm, labels_in, c_sem.at[2])
+    c_copy = pltpu.make_async_copy(centers_hbm, cen, c_sem.at[0])
+    feat_fetch.start()
+    labels_fetch.start()
     for i in range(N_W):
         w_copy(i).start()
     c_copy.start()
 
     barrier = pltpu.get_barrier_semaphore()
     for axis in range(3):
-        for k in (1, 2, 3):
+        for k in (2, 1, 3):
             pl.semaphore_signal(barrier, inc=1, device_id=peer(axis, k), device_id_type=MESH)
     pl.semaphore_signal(barrier, inc=1, device_id=peer(3, 1), device_id_type=MESH)
 
+    labels_fetch.wait()
     lane = lax.broadcasted_iota(jnp.int32, (16, 128), 1)
     for c in range(2):
         low = labels_in[...]
@@ -107,12 +112,12 @@
             line = jnp.where(lane[0:1] < 64, low[2 * g : 2 * g + 1], high[2 * g + 1 : 2 * g + 2])
             labels[2 * c + g // 4 : 2 * c + g // 4 + 1, (g % 4) * 128 : (g % 4 + 1) * 128] = line
 
+    feat_fetch.wait()
     acc = jnp.zeros((OWN, D), f32)
     for i in range(N_W):
         w_copy(i).wait()
-        acc = acc + plain_dot(
-            feat[:, i * W_CHUNK : (i + 1) * W_CHUNK], E[i // 2, (i % 2) * 2048 : (i % 2) * 2048 + W_CHUNK]
-        )
+        at = (i % 2) * 2048
+        acc = acc + plain_dot(feat[:, i * W_CHUNK : (i + 1) * W_CHUNK], E[i // 2, at : at + W_CHUNK])
     own = acc.astype(bf16).astype(f32)
     own_inv = lax.rsqrt(jnp.sum(own * own, axis=1, keepdims=True) + epsilon)
     own_emb[...] = own
@@ -146,14 +151,14 @@
 
     def ag_start(buf, inst, p, s):
         def act(order):
-            for k in (1, 2, 3):
+            for k in (2, 1, 3):
                 ag_copy(buf, inst, p, s, k, order).start()
 
         by_order(p, act)
 
     def ag_next(buf, inst, s):
         for p in range(4):
-            for k in (1, 2, 3):
+            for k in (2, 1, 3):
                 ag_copy(buf, inst, p, s, k, ORDERS[p]).wait_recv()
             if s < 2:
                 ag_start(buf, inst, p, s + 1)
@@ -162,7 +167,7 @@
 
     def ag_drain(buf, inst):
         for s in range(3):
-            for k in (1, 2, 3):
+            for k in (2, 1, 3):
                 for p in range(4):
                     ag_copy(buf, inst, p, s, k, ORDERS[p]).wait_send()
 
@@ -243,43 +248,51 @@
 
     rows[...] = jnp.zeros_like(rows)
     n_a = CLASSES // JA
-    tiles = 4 * n_a
-
-    def tile_at(t):
-        bt = lax.rem(t // n_a + 2 * core, 4)
-        return bt, pl.multiple_of(lax.rem(t, n_a) * JA, JA)
-
-    def cosine_tile(t, slot):
-        bt, j0 = tile_at(t)
-        gt[2 * slot : 2 * slot + 2] = last_dims(clow[pl.ds(j0, JA), :], block(emb, bt)).reshape(2, BT, BT)
-
-    def exp_tile(t, slot):
-        bt, j0 = tile_at(t)
-        cosines = gt[2 * slot : 2 * slot + 2].reshape(JA, BT)
-        lab = labels[pl.ds(bt, 1), :] - offset - j0
+
+    def side(n):
+        return lax.rem(n + 2 * core, 4)
+
+    def turn(n):
+        emb_t[side(n)] = transposed(block(emb, side(n)))
+
+    def cosine_tile(n, a):
+        slot = 2 * (a % 2)
+        gt[slot : slot + 2] = plain_dot(clow[a * JA : (a + 1) * JA, :], emb_t[side(n)]).reshape(2, BT, BT)
+
+    def exp_tile(n, a):
+        slot = 2 * (a % 2)
+        cosines = gt[slot : slot + 2].reshape(JA, BT)
+        lab = labels[pl.ds(side(n), 1), :] - offset - a * JA
         hot = lab == lax.broadcasted_iota(jnp.int32, (JA, BT), 0)
         e = jnp.where(hot, 0.0, jnp.exp2(cosines * exp2_scale))
-        rows[bt] += jnp.sum(e.reshape(JA // 8, 8, BT), axis=0)
-        E[bt, pl.ds(j0, JA), :] = e.astype(bf16)
-
+        rows[side(n)] += jnp.sum(e.reshape(JA // 8, 8, BT), axis=0)
+        E[side(n), a * JA : (a + 1) * JA, :] = e.astype(bf16)
+
+    turn(0)
+    turn(1)
     cosine_tile(0, 0)
 
-    @pl.loop(0, tiles // 2 - 1)
-    def _(m):
-        @pl.when(m == tiles // 4 - 1)
+    @pl.loop(0, 3)
+    def _(n):
+        @pl.when(n == 1)
         def _():
             pair_wait(emb, 0)
-
-        for u in range(9):
-            feature_copy(m * 9 + u + 1).start()
-        cosine_tile(2 * m + 1, 1)
-        exp_tile(2 * m, 0)
-        cosine_tile(2 * m + 2, 0)
-        exp_tile(2 * m + 1, 1)
-
-    cosine_tile(tiles - 1, 1)
-    exp_tile(tiles - 2, 0)
-    exp_tile(tiles - 1, 1)
+            turn(2)
+            turn(3)
+
+        for u in range(21):
+            feature_copy(n * 21 + u + 1).start()
+        for a in range(n_a):
+            if a + 1 < n_a:
+                cosine_tile(n, a + 1)
+            else:
+                cosine_tile(n + 1, 0)
+            exp_tile(n, a)
+
+    for a in range(n_a):
+        if a + 1 < n_a:
+            cosine_tile(3, a + 1)
+        exp_tile(3, a)
 
     def margin(tc):
         ts = jnp.sqrt(1.0 - tc * tc)
@@ -298,16 +311,15 @@
         bt = 2 * core + h
         rows_t = tt[bt].astype(f32) + ttr[h].astype(f32)
         ttr[h] = rows_t.astype(bf16)
-        own_rows = jnp.concatenate([emb[p, core, 2 * h : 2 * h + 2].reshape(BT, 128) for p in range(4)], axis=1)
-        tc = jnp.sum(transposed(own_rows).astype(f32) * rows_t, axis=0, keepdims=True)
+        tc = jnp.sum(emb_t[bt].astype(f32) * rows_t, axis=0, keepdims=True)
         margined, _ = margin(tc)
         ar_send[0, pl.ds(bt, 1), :] += jnp.where(on_chip(bt), jnp.exp(margined), 0.0)
         ar_send[0, pl.ds(4 + bt, 1), :] = tc
 
     AR_PEERS = (
-        tuple((z, c) for z in range(4) for c in range(2) if z + c > 0),
-        tuple((1, k) for k in (1, 2, 3)),
-        tuple((0, k) for k in (1, 2, 3)),
+        tuple((z, c) for z in (2, 1, 3, 0) for c in range(2) if z + c > 0),
+        tuple((1, k) for k in (2, 1, 3)),
+        tuple((0, k) for k in (2, 1, 3)),
     )
 
     def ar_copy(s, n):
@@ -373,7 +385,7 @@
     for bt in range(4):
         total = ar_send[3, bt : bt + 1, :]
         margined, slope = margin(ar_send[3, 4 + bt : 5 + bt, :])
-        loss_out[bt : bt + 1, :] = jnp.log(total) - margined
+        losses[bt : bt + 1, :] = jnp.log(total) - margined
         scale = logit_scale / total
         rows[bt, 0:1, :] = scale
         rows[bt, 1:2, :] = (jnp.exp(margined) - total) * slope * scale
@@ -408,7 +420,7 @@
 
     def rs_start(s, p):
         def act(order):
-            for k in (1, 2, 3):
+            for k in (2, 1, 3):
                 rs_copy(s, p, k, order).start()
 
         by_order(p, act)
@@ -416,7 +428,7 @@
     def rs_step(s):
         bufs = (rb1, rb2, rb3)[s]
         for p in range(4):
-            for k in (1, 2, 3):
+            for k in (2, 1, 3):
                 rs_copy(s, p, k, ORDERS[p]).wait_recv()
 
             def act(order):
@@ -428,7 +440,7 @@
                 else:
                     total = gs3[p, me[axis]]
                 total = total.astype(f32)
-                for k in (1, 2, 3):
+                for k in (2, 1, 3):
                     total = total + bufs[p, k - 1].astype(f32)
                 if s == 0:
                     gs2[p] = total.astype(bf16)
@@ -437,7 +449,7 @@
                 else:
                     rs_out[:, p * 128 : (p + 1) * 128] = total
                 if s < 2:
-                    for k in (1, 2, 3):
+                    for k in (2, 1, 3):
                         rs_copy(s + 1, p, k, order).start()
 
             by_order(p, act)
@@ -456,14 +468,10 @@
     for p in range(4):
         rs_start(0, p)
 
-    def out_copy(i):
-        r = pl.ds(pl.multiple_of(i * JC, JC), JC)
-        return pltpu.make_async_copy(clow.at[r], gc_hbm.at[r], out_sem.at[i])
-
     steps = {
-        3: functools.partial(rs_step, 0),
-        5: functools.partial(rs_step, 1),
-        6: owner_step,
+        2: functools.partial(rs_step, 0),
+        4: functools.partial(rs_step, 1),
+        5: owner_step,
         7: functools.partial(ag_next, gemb, 1, 0),
     }
 
@@ -473,7 +481,7 @@
         cf = cen[r, :].astype(f32)
         inv = lax.rsqrt(jnp.sum(cf * cf, axis=1, keepdims=True) + epsilon)
         along = jnp.sum(gu * cf, axis=1, keepdims=True) * (inv * inv * inv)
-        clow[r, :] = (gu * inv - cf * along).astype(bf16)
+        gc_out[r, :] = (gu * inv - cf * along).astype(bf16)
 
     @pl.loop(0, CLASSES // JC)
     def _(i):
@@ -490,17 +498,21 @@
         before = jnp.maximum(i - 1, 0)
         finish_centers(before, lax.rem(i + 1, 2))
 
-        @pl.when(i > 0)
-        def _():
-            out_copy(before).start()
-
         for at, step in steps.items():
             @pl.when(i == at)
             def _():
                 step()
 
     finish_centers(CLASSES // JC - 1, (CLASSES // JC - 1) % 2)
-    out_copy(CLASSES // JC - 1).start()
+    position = core * (N // 2) + chip
+    line = jnp.zeros((1, BT), f32)
+    for bt in range(4):
+        line = jnp.where(position // 32 == bt, losses[bt : bt + 1, :], line)
+    line = jnp.broadcast_to(line, (8, BT))
+    for bit in (1, 2, 4, 8, 16):
+        moved = pltpu.roll(line, BT - bit * OWN, 1)
+        line = jnp.where(lax.rem(position // bit, 2) == 1, moved, line)
+    loss_out[...] = line[:, 0:128]
 
     ag_next(gemb, 1, 1)
 
@@ -527,58 +539,34 @@
     )
     fc_copy.start()
     fc_copy.wait()
-    fc_out[...] = (fc[0:104] + fc_recv[...])[0:F_DEV]
-
-    for i in range(CLASSES // JC):
-        out_copy(i).wait()
+    fc_out[...] = fc[0:104] + fc_recv[...]
+
     ag_drain(emb, 0)
     ag_drain(gemb, 1)
     for s in range(3):
         for p in range(4):
-            for k in (1, 2, 3):
+            for k in (2, 1, 3):
                 rs_copy(s, p, k, ORDERS[p]).wait_send()
-
-
-def emit_kernel(loss_all, fc, gc_hbm, loss_out, fc_out, out_hbm, held, in_sem, out_sem):
-    step = CLASSES // 8
-
-    def read(i):
-        r = pl.ds(i * step, step)
-        return pltpu.make_async_copy(gc_hbm.at[r], held.at[r], in_sem.at[i])
-
-    def write(i):
-        r = pl.ds(i * step, step)
-        return pltpu.make_async_copy(held.at[r], out_hbm.at[r], out_sem.at[i])
-
-    for i in range(8):
-        read(i).start()
-    chip = (lax.axis_index("cls_0") * 4 + lax.axis_index("cls_1")) * 4 + lax.axis_index("cls_2")
-    position = lax.axis_index("cls_3") * 64 + chip
-    line = loss_all[pl.ds(position // 32, 1), :]
-    loss_out[...] = pltpu.roll(line, lax.rem(BT - lax.rem(position, 32) * OWN, BT), 1)[:, 0:OWN]
-    fc_out[...] = fc[...]
-    for i in range(8):
-        read(i).wait()
-        write(i).start()
-    for i in range(8):
-        write(i).wait()
 
 
 def on_device(features, fc_weight, centers, labels):
     vmem = pl.BlockSpec(memory_space=pltpu.VMEM)
     anywhere = pl.BlockSpec(memory_space=pl.ANY)
     dma = pltpu.SemaphoreType.DMA
-    loss_all, grad_fc, grad_centers = pl.pallas_call(
+    loss, grad_fc, grad_centers = pl.pallas_call(
         kernel,
         out_shape=(
-            jax.ShapeDtypeStruct((4, BT), f32),
-            jax.ShapeDtypeStruct((F_DEV, D), f32),
-            jax.ShapeDtypeStruct((CLASSES, D), bf16),
+            pltpu.VMEM((8, 128), f32),
+            pltpu.VMEM((104, D), f32),
+            pltpu.VMEM((CLASSES, D), bf16),
         ),
-        in_specs=[vmem, anywhere, anywhere, vmem],
-        out_specs=(vmem, vmem, anywhere),
+        in_specs=[anywhere] * 4,
+        out_specs=(vmem, vmem, vmem),
         scratch_shapes=[
+            pltpu.VMEM((OWN, F), bf16),
+            pltpu.VMEM((16, 128), jnp.int32),
             pltpu.VMEM((4, BT), jnp.int32),
+            pltpu.VMEM((8, BT), f32),
             pltpu.VMEM((4, CLASSES, BT), bf16),
             pltpu.VMEM((CLASSES, D), bf16),
             pltpu.VMEM((CLASSES, D), bf16),
@@ -586,6 +574,7 @@
             pltpu.VMEM((4, D, BT), bf16),
             pltpu.VMEM((2, D, BT), bf16),
             pltpu.VMEM((4, 2, 4, 4, 4, OWN, 128), bf16),
+            pltpu.VMEM((4, D, BT), bf16),
             pltpu.VMEM((4, 2, 4, 4, 4, OWN, 128), bf16),
             pltpu.VMEM((4, D, BT), f32),
             pltpu.VMEM((2, D, BT), bf16),
@@ -606,8 +595,7 @@
             pltpu.VMEM((3, 7, 8, BT), f32),
             pltpu.VMEM((4, 8, BT), f32),
             dma((N_W,)),
-            dma,
-            dma((CLASSES // JC,)),
+            dma((3,)),
             dma((2, 4, 3, 3)),
             dma((2, 4, 3, 3)),
             dma((3, 4)),
@@ -620,21 +608,10 @@
             dma,
         ],
         compiler_params=pltpu.CompilerParams(
-            collective_id=0, has_side_effects=True, vmem_limit_bytes=66_000_000
+            collective_id=0, has_side_effects=True, vmem_limit_bytes=58_000_000
         ),
     )(features, fc_weight, centers, labels.reshape(16, 128))
-    loss, grad_fc, grad_centers = pl.pallas_call(
-        emit_kernel,
-        out_shape=(
-            jax.ShapeDtypeStruct((1, OWN), f32),
-            jax.ShapeDtypeStruct((F_DEV, D), f32),
-            jax.ShapeDtypeStruct((CLASSES, D), bf16),
-        ),
-        in_specs=[vmem, vmem, anywhere],
-        out_specs=(vmem, vmem, anywhere),
-        scratch_shapes=[pltpu.VMEM((CLASSES, D), bf16), dma((8,)), dma((8,))],
-    )(loss_all, grad_fc, grad_centers)
-    return (loss.reshape(-1), grad_centers, grad_fc)
+    return (loss[0, :OWN], grad_centers, grad_fc[:F_DEV])
 
 
 def solution(mesh):

time: 93 us -> 86.5 us (0.930)
  Pallas kernels: 92.2 us -> 82.5 us
  local copies, waits for them, and re-layouts: 0 us -> 3.21 us
    pallas_call x2 -> x1, Pallas kernels: 92.2 us -> 82.5 us  [on_device(): pl.pallas_call(kernel, out_shape=(pltpu.VMEM((8, 128), f32), pltpu.VMEM((...]
    unnamed x0 -> x2, local copies, waits for them, and re-layouts: none -> 2.69 us
where the time goes in v4:
time: 86.5 us; the launch traced here: 86.4 us
  Pallas kernels  82.5 us (95%)
  local copies, waits for them, and re-layouts  3.21 us (4%)
    pallas_call x1, Pallas kernels, on_device(): pl.pallas_call(kernel, out_shape=(pltpu.VMEM((8, 128), f32), pltpu.VMEM((...  82.5 us
    unnamed x2, local copies, waits for them, and re-layouts  2.69 us

profile of v4, /device:TPU:1, one launch (start us, length us, event | category | flops | bytes accessed | tf_op | source)
XLA Modules:
  0.0 86.4 jit_solution(2635364438306094107)
XLA Ops:
  0.6 82.5 %shard_map.67 = (f32[8,128]{1,0:T(8,128)S(1)}, f32[104,512]{1,0:T(8,128)S(1)}, bf16[4096,512]{1,0:T(8,128)(2,1)S(1)}) custom-call(bf16[16,12544]{1,0:T(8,128)(2,1)} %feat_hbm.1, bf16[12544,512]{1,0:T(8,128)(2,1)} %w_hbm.1, bf16[4096,512]{1,0:T(8,128)(2,1)} %centers_hbm.1, s32[16,128]{1,0:T(8,128)} %bitcast.5), custom_call_target="tpu_custom_call" | custom-call | tf_op jit(solution)/shard_map/pallas_call | solution.py:556
  83.2 0.5 slice_bitcast_fusion
  83.7 2.0 %copy.9 = bf16[4096,512]{1,0:T(8,128)(2,1)} copy(bf16[4096,512]{1,0:T(8,128)(2,1)S(1)} %get-tuple-element.10) | data formatting | bytes 8388608
  85.7 0.7 copy.10

commit v5 on v4

--- a/solution.py
+++ b/solution.py
@@ -61,8 +61,8 @@
     feat_hbm, w_hbm, centers_hbm, labels_hbm,
     loss_out, fc_out, gc_out,
     feat, labels_in, labels, losses,
-    E, cen, clow, ct, tt, ttr, emb, emb_t, gemb, gt, gsend, grecv, gs, rb1, gs2, rb2, gs3, rb3, rs_out, cols,
-    cols_t, fc_send, fc_recv, own_emb, ar_send, ar_recv, rows,
+    E, cen, clow, ct, tt, ttr, emb, emb_t, gemb, gt, gsend, grecv, gs, rb1, gs2, rb2, gs3, rb3, cols,
+    cols_t, fc_send, fc_recv, ar_send, ar_recv, rows,
     w_sem, c_sem, ag_send, ag_recv, d_send, d_recv, rs_send, rs_recv,
     s_send, s_recv, a_send, a_recv,
 ):
@@ -120,7 +120,6 @@
         acc = acc + plain_dot(feat[:, i * W_CHUNK : (i + 1) * W_CHUNK], E[i // 2, at : at + W_CHUNK])
     own = acc.astype(bf16).astype(f32)
     own_inv = lax.rsqrt(jnp.sum(own * own, axis=1, keepdims=True) + epsilon)
-    own_emb[...] = own
     own_low = (own * own_inv).astype(bf16)
 
     def put_own(buf, value):
@@ -166,7 +165,7 @@
                 pair_copy(buf, inst, p).start()
 
     def ag_drain(buf, inst):
-        for s in range(3):
+        for s in range(inst, 3):
             for k in (2, 1, 3):
                 for p in range(4):
                     ag_copy(buf, inst, p, s, k, ORDERS[p]).wait_send()
@@ -191,6 +190,8 @@
     pl.semaphore_wait(barrier, 10)
     for p in range(4):
         ag_start(emb, 0, p, 0)
+
+    feat[...] = (feat[...].astype(f32) * own_inv).astype(bf16)
 
     c_copy.wait()
 
@@ -203,7 +204,7 @@
         clow[r, :] = low
         ct[:, r] = transposed(low)
 
-        @pl.when(i == 4)
+        @pl.when(i == 5)
         def _():
             ag_next(emb, 0, 0)
 
@@ -410,7 +411,7 @@
             src = gs2.at[(p,) + tuple(to[a] if a == axis else slice(None) for a in left)]
             dst = rb2.at[p, k - 1]
         else:
-            src = gs3.at[p, to[axis]]
+            src = gs3.at[p]
             dst = rb3.at[p, k - 1]
         return pltpu.make_async_remote_copy(
             src_ref=src, dst_ref=dst,
@@ -438,7 +439,7 @@
                 elif s == 1:
                     total = gs2[(p,) + tuple(me[a] if a == axis else slice(None) for a in sorted(order[:2]))]
                 else:
-                    total = gs3[p, me[axis]]
+                    total = gs3[p]
                 total = total.astype(f32)
                 for k in (2, 1, 3):
                     total = total + bufs[p, k - 1].astype(f32)
@@ -447,32 +448,24 @@
                 elif s == 1:
                     gs3[p] = total.astype(bf16)
                 else:
-                    rs_out[:, p * 128 : (p + 1) * 128] = total
-                if s < 2:
-                    for k in (2, 1, 3):
+                    where = tuple(slice(None) if a == axis else me[a] for a in range(3))
+                    gemb[(p, core) + where] = total.astype(bf16)
+                for k in (2, 1, 3):
+                    if s < 2:
                         rs_copy(s + 1, p, k, order).start()
+                    else:
+                        ag_copy(gemb, 1, p, 1, k, order).start()
 
             by_order(p, act)
-
-    def owner_step():
-        rs_step(2)
-        grad_dir = rs_out[...]
-        own = own_emb[...]
-        inv = lax.rsqrt(jnp.sum(own * own, axis=1, keepdims=True) + epsilon)
-        direction = own * inv
-        along = jnp.sum(grad_dir * direction, axis=1, keepdims=True)
-        put_own(gemb, ((grad_dir - direction * along) * inv).astype(bf16))
-        for p in range(4):
-            ag_start(gemb, 1, p, 0)
 
     for p in range(4):
         rs_start(0, p)
 
     steps = {
         2: functools.partial(rs_step, 0),
-        4: functools.partial(rs_step, 1),
-        5: owner_step,
-        7: functools.partial(ag_next, gemb, 1, 0),
+        3: functools.partial(rs_step, 1),
+        5: functools.partial(rs_step, 2),
+        7: functools.partial(ag_next, gemb, 1, 1),
     }
 
     def finish_centers(i, slot):
@@ -514,8 +507,6 @@
         line = jnp.where(lax.rem(position // bit, 2) == 1, moved, line)
     loss_out[...] = line[:, 0:128]
 
-    ag_next(gemb, 1, 1)
-
     others = cols.at[pl.ds(0, N // 2 - 1)]
     pltpu.make_async_copy(others, others, a_send).wait()
     pltpu.make_async_copy(others, others, a_recv).wait()
@@ -528,18 +519,27 @@
         cols_t[h] = last_dims(pick, cols[h * 32 : (h + 1) * 32].reshape(BT, 384)).astype(bf16)
 
     ag_next(gemb, 1, 2)
-    fc = jnp.zeros((208, D), f32)
+    tangents = []
     for h in range(2):
-        rows_h = jnp.concatenate([gemb[p, core, 2 * h : 2 * h + 2].reshape(BT, 128) for p in range(4)], axis=1)
-        fc = fc + plain_dot(cols_t[h], rows_h)
-    fc_send[...] = fc[104:208]
+        grad, low = (
+            jnp.concatenate([buf[p, core, 2 * h : 2 * h + 2].reshape(BT, 128) for p in range(4)], axis=1).astype(f32)
+            for buf in (gemb, emb)
+        )
+        along = jnp.sum(grad * low, axis=1, keepdims=True)
+        tangents.append((grad - low * along).astype(bf16))
+
+    def fc_rows(start):
+        return sum(plain_dot(cols_t[h, start : start + 104], tangents[h]) for h in range(2))
+
+    fc_send[...] = fc_rows(104)
     fc_copy = pltpu.make_async_remote_copy(
         src_ref=fc_send, dst_ref=fc_recv, send_sem=d_send.at[1, 0], recv_sem=d_recv.at[1, 0],
         device_id=peer(3, 1), device_id_type=MESH,
     )
     fc_copy.start()
+    fc_own = fc_rows(0)
     fc_copy.wait()
-    fc_out[...] = fc[0:104] + fc_recv[...]
+    fc_out[...] = fc_own + fc_recv[...]
 
     ag_drain(emb, 0)
     ag_drain(gemb, 1)
@@ -584,13 +584,11 @@
             pltpu.VMEM((4, 4, 4, OWN, 128), bf16),
             pltpu.VMEM((4, 3, 4, OWN, 128), bf16),
             pltpu.VMEM((4, 4, OWN, 128), bf16),
-            pltpu.VMEM((4, 3, OWN, 128), bf16),
-            pltpu.VMEM((OWN, D), f32),
+            pltpu.VMEM((4, 3, 4, OWN, 128), bf16),
             pltpu.VMEM((N // 2, OWN, 384), bf16),
             pltpu.VMEM((2, 208, BT), bf16),
             pltpu.VMEM((104, D), f32),
             pltpu.VMEM((104, D), f32),
-            pltpu.VMEM((OWN, D), f32),
             pltpu.VMEM((4, 8, BT), f32),
             pltpu.VMEM((3, 7, 8, BT), f32),
             pltpu.VMEM((4, 8, BT), f32),

time: 86.5 us -> 83.2 us (0.962)
  Pallas kernels: 82.5 us -> 79.2 us
    pallas_call x1, Pallas kernels: 82.5 us -> 79.2 us  [on_device(): pl.pallas_call(kernel, out_shape=(pltpu.VMEM((8, 128), f32), pltpu.VMEM((...]
where the time goes in v5:
time: 83.2 us; the launch traced here: 83.1 us
  Pallas kernels  79.2 us (95%)
  local copies, waits for them, and re-layouts  3.21 us (4%)
    pallas_call x1, Pallas kernels, on_device(): pl.pallas_call(kernel, out_shape=(pltpu.VMEM((8, 128), f32), pltpu.VMEM((...  79.2 us
    unnamed x2, local copies, waits for them, and re-layouts  2.69 us

profile of v5, /device:TPU:1, one launch (start us, length us, event | category | flops | bytes accessed | tf_op | source)
XLA Modules:
  0.0 83.1 jit_solution(4883478144504721816)
XLA Ops:
  0.6 79.2 %shard_map.67 = (f32[8,128]{1,0:T(8,128)S(1)}, f32[104,512]{1,0:T(8,128)S(1)}, bf16[4096,512]{1,0:T(8,128)(2,1)S(1)}) custom-call(bf16[16,12544]{1,0:T(8,128)(2,1)} %feat_hbm.1, bf16[12544,512]{1,0:T(8,128)(2,1)} %w_hbm.1, bf16[4096,512]{1,0:T(8,128)(2,1)} %centers_hbm.1, s32[16,128]{1,0:T(8,128)} %bitcast.5), custom_call_target="tpu_custom_call" | custom-call | tf_op jit(solution)/shard_map/pallas_call | solution.py:556
  79.9 0.5 slice_bitcast_fusion
  80.4 2.0 %copy.9 = bf16[4096,512]{1,0:T(8,128)(2,1)} copy(bf16[4096,512]{1,0:T(8,128)(2,1)S(1)} %get-tuple-element.10) | data formatting | bytes 8388608
  82.4 0.7 copy.10

commit v6 on v5

--- a/solution.py
+++ b/solution.py
@@ -131,6 +131,9 @@
         where = tuple(slice(None) if a in gathered else at[a] for a in range(3))
         return buf.at[(p, core) + where]
 
+    def wait_bytes(ref, sem):
+        pltpu.make_async_copy(ref, ref, sem).wait()
+
     def by_order(p, act):
         if p < 3:
             act(ORDERS[p])
@@ -144,7 +147,7 @@
         v = view(buf, p, order[:s])
         return pltpu.make_async_remote_copy(
             src_ref=v, dst_ref=v,
-            send_sem=ag_send.at[inst, p, s, k - 1], recv_sem=ag_recv.at[inst, p, s, k - 1],
+            send_sem=ag_send.at[inst, s], recv_sem=ag_recv.at[inst, p, s],
             device_id=peer(order[s], k), device_id_type=MESH,
         )
 
@@ -157,18 +160,17 @@
 
     def ag_next(buf, inst, s):
         for p in range(4):
-            for k in (2, 1, 3):
-                ag_copy(buf, inst, p, s, k, ORDERS[p]).wait_recv()
+            first = buf.at[p, 0]
+            wait_bytes((first.at[0, 0, 0:3], first.at[0, 0:3], first.at[0:3])[s], ag_recv.at[inst, p, s])
             if s < 2:
                 ag_start(buf, inst, p, s + 1)
             elif inst == 0:
                 pair_copy(buf, inst, p).start()
 
     def ag_drain(buf, inst):
+        sizes = (buf.at[:, 0, 0, 0, 0:3], buf.at[:, 0, 0, 0:3], buf.at[:, 0, 0:3])
         for s in range(inst, 3):
-            for k in (2, 1, 3):
-                for p in range(4):
-                    ag_copy(buf, inst, p, s, k, ORDERS[p]).wait_send()
+            wait_bytes(sizes[s], ag_send.at[inst, s])
 
     def pair_copy(buf, inst, p):
         v = buf.at[p, core]
@@ -331,7 +333,7 @@
             to = peer(*AR_PEERS[s][n])
         return pltpu.make_async_remote_copy(
             src_ref=ar_send.at[s], dst_ref=ar_recv.at[s, n],
-            send_sem=s_send.at[s, n], recv_sem=s_recv.at[s, n],
+            send_sem=s_send.at[s], recv_sem=s_recv.at[s],
             device_id=to, device_id_type=MESH,
         )
 
@@ -341,8 +343,8 @@
 
     def ar_finish(s):
         total = ar_send[s]
+        wait_bytes(ar_recv.at[s, 0 : len(AR_PEERS[s])], s_recv.at[s])
         for n in range(len(AR_PEERS[s])):
-            ar_copy(s, n).wait_recv()
             total = total + ar_recv[s, n]
         ar_send[s + 1] = total
         if s < 2:
@@ -380,8 +382,7 @@
 
     ar_finish(2)
     for s in range(3):
-        for n in range(len(AR_PEERS[s])):
-            ar_copy(s, n).wait_send()
+        wait_bytes(ar_recv.at[s, 0 : len(AR_PEERS[s])], s_send.at[s])
 
     for bt in range(4):
         total = ar_send[3, bt : bt + 1, :]
@@ -415,7 +416,7 @@
             dst = rb3.at[p, k - 1]
         return pltpu.make_async_remote_copy(
             src_ref=src, dst_ref=dst,
-            send_sem=rs_send.at[s, p, k - 1], recv_sem=rs_recv.at[s, p, k - 1],
+            send_sem=rs_send.at[s], recv_sem=rs_recv.at[s, p],
             device_id=to, device_id_type=MESH,
         )
 
@@ -429,8 +430,7 @@
     def rs_step(s):
         bufs = (rb1, rb2, rb3)[s]
         for p in range(4):
-            for k in (2, 1, 3):
-                rs_copy(s, p, k, ORDERS[p]).wait_recv()
+            wait_bytes(bufs.at[p], rs_recv.at[s, p])
 
             def act(order):
                 axis = order[2 - s]
@@ -544,9 +544,7 @@
     ag_drain(emb, 0)
     ag_drain(gemb, 1)
     for s in range(3):
-        for p in range(4):
-            for k in (2, 1, 3):
-                rs_copy(s, p, k, ORDERS[p]).wait_send()
+        wait_bytes((rb1, rb2, rb3)[s], rs_send.at[s])
 
 
 def on_device(features, fc_weight, centers, labels):
@@ -565,7 +563,7 @@
         scratch_shapes=[
             pltpu.VMEM((OWN, F), bf16),
             pltpu.VMEM((16, 128), jnp.int32),
-            pltpu.VMEM((4, BT), jnp.int32),
+            pltpu.VMEM((16, BT), jnp.int32),
             pltpu.VMEM((8, BT), f32),
             pltpu.VMEM((4, CLASSES, BT), bf16),
             pltpu.VMEM((CLASSES, D), bf16),
@@ -594,14 +592,14 @@
             pltpu.VMEM((4, 8, BT), f32),
             dma((N_W,)),
             dma((3,)),
-            dma((2, 4, 3, 3)),
-            dma((2, 4, 3, 3)),
+            dma((2, 3)),
+            dma((2, 4, 3)),
             dma((3, 4)),
             dma((3, 4)),
-            dma((3, 4, 3)),
-            dma((3, 4, 3)),
-            dma((3, 7)),
-            dma((3, 7)),
+            dma((3,)),
+            dma((3, 4)),
+            dma((3,)),
+            dma((3,)),
             dma,
             dma,
         ],

time: 83.2 us -> 81 us (0.974)
  Pallas kernels: 79.2 us -> 77 us
    pallas_call x1, Pallas kernels: 79.2 us -> 77 us  [on_device(): pl.pallas_call(kernel, out_shape=(pltpu.VMEM((8, 128), f32), pltpu.VMEM((...]
where the time goes in v6:
time: 81 us; the launch traced here: 80.9 us
  Pallas kernels  77 us (95%)
  local copies, waits for them, and re-layouts  3.21 us (4%)
    pallas_call x1, Pallas kernels, on_device(): pl.pallas_call(kernel, out_shape=(pltpu.VMEM((8, 128), f32), pltpu.VMEM((...  77 us
    unnamed x2, local copies, waits for them, and re-layouts  2.69 us

profile of v6, /device:TPU:1, one launch (start us, length us, event | category | flops | bytes accessed | tf_op | source)
XLA Modules:
  0.0 80.9 jit_solution(10673136627460943607)
XLA Ops:
  0.6 77.0 %shard_map.67 = (f32[8,128]{1,0:T(8,128)S(1)}, f32[104,512]{1,0:T(8,128)S(1)}, bf16[4096,512]{1,0:T(8,128)(2,1)S(1)}) custom-call(bf16[16,12544]{1,0:T(8,128)(2,1)} %feat_hbm.1, bf16[12544,512]{1,0:T(8,128)(2,1)} %w_hbm.1, bf16[4096,512]{1,0:T(8,128)(2,1)} %centers_hbm.1, s32[16,128]{1,0:T(8,128)} %bitcast.5), custom_call_target="tpu_custom_call" | custom-call | tf_op jit(solution)/shard_map/pallas_call | solution.py:554
  77.7 0.5 slice_bitcast_fusion
  78.2 2.0 %copy.9 = bf16[4096,512]{1,0:T(8,128)(2,1)} copy(bf16[4096,512]{1,0:T(8,128)(2,1)S(1)} %get-tuple-element.10) | data formatting | bytes 8388608
  80.2 0.7 copy.10

commit v7 on v6

--- a/solution.py
+++ b/solution.py
@@ -176,13 +176,13 @@
         v = buf.at[p, core]
         return pltpu.make_async_remote_copy(
             src_ref=v, dst_ref=v,
-            send_sem=d_send.at[inst, p], recv_sem=d_recv.at[inst, p],
+            send_sem=d_send.at[0], recv_sem=d_recv.at[0],
             device_id=peer(3, 1), device_id_type=MESH,
         )
 
     def pair_wait(buf, inst):
-        for p in range(4):
-            pair_copy(buf, inst, p).wait()
+        wait_bytes(buf.at[:, 0], d_send.at[0])
+        wait_bytes(buf.at[:, 0], d_recv.at[0])
 
     def block(buf, bt):
         c, y0 = bt // 2, (bt % 2) * 2
@@ -229,12 +229,12 @@
     def tt_copy():
         return pltpu.make_async_remote_copy(
             src_ref=tt.at[pl.ds(2 * (1 - core), 2)], dst_ref=ttr,
-            send_sem=d_send.at[1, 1], recv_sem=d_recv.at[1, 1], device_id=peer(3, 1), device_id_type=MESH,
+            send_sem=d_send.at[1], recv_sem=d_recv.at[1], device_id=peer(3, 1), device_id_type=MESH,
         )
 
     tt_copy().start()
     def tile_of(c):
-        return jnp.minimum((c * 2 * F_DEV) // 128, F // 128 - 3)
+        return jnp.minimum(lax.div(c * (2 * F_DEV), 128), F // 128 - 3)
 
     def feature_copy(k):
         to = lax.bitwise_and(chip + k, N // 2 - 1)
@@ -355,7 +355,7 @@
     def g_copy(h):
         return pltpu.make_async_remote_copy(
             src_ref=gsend.at[h], dst_ref=grecv.at[h],
-            send_sem=d_send.at[2, h], recv_sem=d_recv.at[2, h], device_id=peer(3, 1), device_id_type=MESH,
+            send_sem=d_send.at[2 + h], recv_sem=d_recv.at[2 + h], device_id=peer(3, 1), device_id_type=MESH,
         )
 
     half = CLASSES // 2
@@ -533,7 +533,7 @@
 
     fc_send[...] = fc_rows(104)
     fc_copy = pltpu.make_async_remote_copy(
-        src_ref=fc_send, dst_ref=fc_recv, send_sem=d_send.at[1, 0], recv_sem=d_recv.at[1, 0],
+        src_ref=fc_send, dst_ref=fc_recv, send_sem=d_send.at[4], recv_sem=d_recv.at[4],
         device_id=peer(3, 1), device_id_type=MESH,
     )
     fc_copy.start()
@@ -594,8 +594,8 @@
             dma((3,)),
             dma((2, 3)),
             dma((2, 4, 3)),
-            dma((3, 4)),
-            dma((3, 4)),
+            dma((5,)),
+            dma((5,)),
             dma((3,)),
             dma((3, 4)),
             dma((3,)),

time: 81 us -> 80.7 us (level)
  no operation moved by 1% of the time
where the time goes in v7:
time: 80.7 us; the launch traced here: 80.6 us
  Pallas kernels  76.8 us (95%)
  local copies, waits for them, and re-layouts  3.21 us (4%)
    pallas_call x1, Pallas kernels, on_device(): pl.pallas_call(kernel, out_shape=(pltpu.VMEM((8, 128), f32), pltpu.VMEM((...  76.8 us
    unnamed x2, local copies, waits for them, and re-layouts  2.69 us

profile of v7, /device:TPU:1, one launch (start us, length us, event | category | flops | bytes accessed | tf_op | source)
XLA Modules:
  0.0 80.6 jit_solution(4711638518237552063)
XLA Ops:
  0.6 76.8 %shard_map.67 = (f32[8,128]{1,0:T(8,128)S(1)}, f32[104,512]{1,0:T(8,128)S(1)}, bf16[4096,512]{1,0:T(8,128)(2,1)S(1)}) custom-call(bf16[16,12544]{1,0:T(8,128)(2,1)} %feat_hbm.1, bf16[12544,512]{1,0:T(8,128)(2,1)} %w_hbm.1, bf16[4096,512]{1,0:T(8,128)(2,1)} %centers_hbm.1, s32[16,128]{1,0:T(8,128)} %bitcast.5), custom_call_target="tpu_custom_call" | custom-call | tf_op jit(solution)/shard_map/pallas_call | solution.py:554
  77.4 0.5 slice_bitcast_fusion
  77.9 2.0 %copy.9 = bf16[4096,512]{1,0:T(8,128)(2,1)} copy(bf16[4096,512]{1,0:T(8,128)(2,1)S(1)} %get-tuple-element.10) | data formatting | bytes 8388608
  79.9 0.7 copy.10
